TPU v7x, 256 devices: a whole 4x4x8 slice. The times are simulated.
256 devices in a mesh: seq: 8 (over x, y_hi), head: 32 (over z, y_lo, core).
Axes of the slice: x: 4, y: 4 (y_hi: 2, y_lo: 2; y = y_hi * 2 + y_lo), z: 8, core: 2. Of those that a mesh axis runs over, the one named last changes fastest.
Arguments:
- xraw: bfloat16 [8192, 8192], P('seq', 'head'), may hold values from -6 to 6
- zgate: bfloat16 [8192, 8192], P('seq', 'head'), may hold values from -6 to 6
- bcraw: bfloat16 [8192, 256], P('seq'), may hold values from -6 to 6
- dt: float32 [128, 8192], P('head', 'seq'), may hold values from 3.0517578e-06 to 0.25, as said below
- a_rate: float32 [128], P('head'), may hold values from 1 to 2
- d_skip: float32 [128], P('head'), may hold values from 0.5 to 1.5
- conv_x: float32 [4, 8192], P(None, 'head'), may hold values from -3 to 3
- conv_bc: float32 [4, 256], replicated, may hold values from -3 to 3
- dout: bfloat16 [8192, 8192], P('seq', 'head'), may hold values from -6 to 6
Outputs:
- x_raw_grad: bfloat16 [8192, 8192], P('seq', 'head')
- gate_grad: bfloat16 [8192, 8192], P('seq', 'head')
- step_grad: float32 [128, 8192], P('head', 'seq')
- bc_raw_grad: float32 [8192, 256], P(('seq', 'head'))
- conv_x_grad: float32 [4, 8192], P(None, 'head')
- conv_bc_grad: float32 [4, 256], replicated
Inputs may be any that keep to these rules, and one draw needn't show every extreme that they name: `dt`: positive step sizes.
All inputs are finite; a program needn't handle non-finite values.
Results may differ from a plain program's by a relative error of at most 0.028.
Values may be sent and summed in bfloat16 or wider, within the bound.
A program may use at most 64 MiB of HBM per device.

v0:
```python
import jax
import jax.numpy as jnp
from jax import lax
from jax.sharding import Mesh
from jax.sharding import PartitionSpec as P

HEAD_DIM = 64
GROUP = 256
CONV = 4
SEQ = ("seq_0", "seq_1")
HEAD = ("head_0", "head_1", "head_2")
SEQ_HEAD = ("seq_0", "seq_1", "head_0", "head_1", "head_2")


def from_behind(value, axis, steps):
    count = lax.axis_size(axis)
    initial, last = (max(0, -steps), min(count, count - steps))
    return lax.ppermute(value, axis, [(source, source + steps) for source in range(initial, last)])


def sent_to_all(x, axis):
    length = lax.axis_size(axis)
    return lax.all_to_all(jnp.broadcast_to(x[None], (length, *x.shape)), axis, 0, 0, tiled=True)


def combined_pairwise(pieces, combine):
    while len(jax.tree.leaves(pieces)[0]) > 1:
        pieces = jax.vmap(combine)(
            *(jax.tree.map(lambda part: part[side::2], pieces) for side in (0, 1))
        )
    return jax.tree.map(lambda part: part[0], pieces)


def prefix(x, axis, combine, identity, reverse):
    length, position = (lax.axis_size(axis), lax.axis_index(axis))
    passed = jnp.arange(length) > position if reverse else jnp.arange(length) < position

    def kept(part, zero, own):
        part = jnp.where(
            passed.reshape(-1, *(1 for _ in own.shape)),
            part.astype(own.dtype),
            jnp.asarray(zero, own.dtype),
        )
        return part[::-1] if reverse else part

    pieces = jax.tree.map(
        lambda part: sent_to_all(part, axis),
        jax.tree.map(lambda part, kind: part.astype(kind), x, (jnp.bfloat16, jnp.bfloat16)),
    )
    return combined_pairwise(jax.tree.map(kept, pieces, identity, x), combine)


def in_blocks(x, dim, length):
    dims = x.shape
    tiles = x.reshape(*dims[:dim], length, dims[dim] // length, *dims[dim + 1 :])
    return jnp.moveaxis(tiles, dim, 0)


def sum_at_owner(x, axis, dim):
    length = lax.axis_size(axis)
    tiles = lax.all_to_all(in_blocks(x, dim, length), axis, 0, 0, tiled=True)
    return jnp.sum(tiles.astype(jnp.float32), axis=0)


def over_copies(x, axis):
    return sent_to_all(x, axis).sum(axis=0)


def by_axis(x, axes):
    for axis in axes:
        x = lax.psum(x, axis)
    return x


def silu_slope(values):
    logistic = jax.nn.sigmoid(values)
    return logistic * (1.0 + values * (1.0 - logistic))


def conv_apply(extended, weight, length):
    conv_len = weight.shape[0]
    running = jnp.zeros((length, extended.shape[1]), jnp.float32)
    for offset in range(conv_len):
        start_row = conv_len - 1 - offset
        running = running + weight[offset][None, :] * extended[
            start_row : start_row + length
        ].astype(jnp.float32)
    return running


def conv_adjoint(extended, weight, length):
    conv_len = weight.shape[0]
    running = jnp.zeros((length, extended.shape[1]), jnp.float32)
    for offset in range(conv_len):
        running = running + weight[offset][None, :] * extended[offset : offset + length]
    return running


def conv_weight_grad(slope_rows, raw_extended, conv_len):
    length = slope_rows.shape[0]
    rows_list = []
    for offset in range(conv_len):
        start_row = conv_len - 1 - offset
        rows_list.append(
            jnp.sum(
                slope_rows * raw_extended[start_row : start_row + length].astype(jnp.float32),
                axis=0,
            )
        )
    return jnp.stack(rows_list)


def combine_states(earlier_part, later_part):
    return (
        earlier_part[0] * later_part[1][:, None, None] + later_part[0],
        earlier_part[1] * later_part[1],
    )


def local(xraw, zgate, bcraw, dt, a_rate, d_skip, conv_x, conv_bc, dout):
    length = xraw.shape[0]
    head_count = a_rate.shape[0]
    head_size = HEAD_DIM
    block_len = GROUP
    block_count = length // block_len
    conv_len = CONV
    state_dim = bcraw.shape[1] // 2
    channels = xraw.shape[1]
    rim_rows = jnp.concatenate(
        [xraw[length - conv_len + 1 :], bcraw[length - conv_len + 1 :]], axis=1
    )
    before = from_behind(rim_rows, SEQ, 1)
    x_extended = jnp.concatenate([before[:, :channels], xraw], axis=0)
    bc_extended = jnp.concatenate([before[:, channels:], bcraw], axis=0)
    x_pre = conv_apply(x_extended, conv_x, length)
    bc_pre = conv_apply(bc_extended, conv_bc, length)
    x_post = jax.nn.silu(x_pre).astype(jnp.bfloat16)
    bc_post = jax.nn.silu(bc_pre).astype(jnp.bfloat16)
    b_blocks = bc_post[:, :state_dim].reshape(block_count, block_len, state_dim)
    c_blocks = bc_post[:, state_dim:].reshape(block_count, block_len, state_dim)
    x_blocks = x_post.reshape(block_count, block_len, head_count, head_size)
    step_sizes = dt.reshape(head_count, block_count, block_len)
    step_t = step_sizes.transpose(1, 2, 0)[..., None]
    x_float = x_blocks.astype(jnp.float32)
    w_blocks = (x_float * step_t).astype(jnp.bfloat16)
    within = jnp.cumsum(a_rate[:, None, None] * step_sizes, axis=2)
    totals = within[..., -1]
    starts = jnp.cumsum(totals, axis=1) - totals
    device_total = jnp.sum(totals, axis=1)
    places = lax.iota(jnp.int32, block_len)
    causal = (places[:, None] >= places[None, :]).astype(jnp.float32)
    decay_pair = jnp.exp(jnp.minimum(within[..., None, :] - within[..., :, None], 0.0)) * causal
    scores = jnp.einsum("ctn,csn->cts", c_blocks, b_blocks, preferred_element_type=jnp.float32)
    kernel = (scores[None] * decay_pair).astype(jnp.bfloat16)
    enter_t = jnp.exp(-within).transpose(1, 2, 0)[..., None]
    leave_t = jnp.exp(-(totals[..., None] - within)).transpose(1, 2, 0)[..., None]
    w_leave = (w_blocks.astype(jnp.float32) * leave_t).astype(jnp.bfloat16)
    ends = jnp.einsum("cshp,csn->hcpn", w_leave, b_blocks, preferred_element_type=jnp.float32)
    gate_vals = zgate.reshape(block_count, block_len, head_count, head_size).astype(jnp.float32)
    upstream = dout.reshape(block_count, block_len, head_count, head_size).astype(jnp.float32)
    dy_bf = (upstream * jax.nn.silu(gate_vals)).astype(jnp.bfloat16)
    dy_float = dy_bf.astype(jnp.float32)
    dy_enter = (dy_float * enter_t).astype(jnp.bfloat16)
    starts_grad = jnp.einsum(
        "cthp,ctn->hcpn", dy_enter, c_blocks, preferred_element_type=jnp.float32
    )
    end_weight = jnp.exp(-(device_total[:, None] - starts - totals))
    local_end = jnp.einsum("hc,hcpn->hpn", end_weight, ends, precision=lax.Precision.HIGHEST)
    local_begin = jnp.einsum(
        "hc,hcpn->hpn", jnp.exp(-starts), starts_grad, precision=lax.Precision.HIGHEST
    )
    device_decay = jnp.exp(-device_total)
    empty_state = jnp.zeros_like(local_end)
    identity = (empty_state, jnp.ones_like(device_decay))
    state_in, unused_decay = prefix((local_end, device_decay), SEQ, combine_states, identity, False)
    grad_out, unused_back = prefix((local_begin, device_decay), SEQ, combine_states, identity, True)
    block_ids = lax.iota(jnp.int32, block_count)
    earlier_mask = (block_ids[:, None] > block_ids[None, :]).astype(jnp.float32)
    into_gap = starts[:, :, None] - starts[:, None, :] - totals[:, None, :]
    into_weight = jnp.exp(-jnp.maximum(into_gap, 0.0)) * earlier_mask
    from_gap = starts[:, None, :] - starts[:, :, None] - totals[:, :, None]
    from_weight = jnp.exp(-jnp.maximum(from_gap, 0.0)) * earlier_mask.T
    states_in = (
        jnp.einsum("hcd,hdpn->hcpn", into_weight, ends, precision=lax.Precision.HIGHEST)
        + jnp.exp(-starts)[..., None, None] * state_in[:, None]
    )
    grads_out = (
        jnp.einsum("hce,hepn->hcpn", from_weight, starts_grad, precision=lax.Precision.HIGHEST)
        + end_weight[..., None, None] * grad_out[:, None]
    )
    states_bf = states_in.astype(jnp.bfloat16)
    grads_bf = grads_out.astype(jnp.bfloat16)
    inner_part = jnp.einsum("hcts,cshp->cthp", kernel, w_blocks, preferred_element_type=jnp.float32)
    outer_part = (
        jnp.einsum("ctn,hcpn->cthp", c_blocks, states_bf, preferred_element_type=jnp.float32)
        * enter_t
    )
    output_y = inner_part + outer_part + d_skip[:, None] * x_float
    gate_grad = (
        (upstream * output_y * silu_slope(gate_vals)).astype(jnp.bfloat16).reshape(length, channels)
    )
    w_grad = jnp.einsum(
        "hcts,cthp->cshp", kernel, dy_bf, preferred_element_type=jnp.float32
    ) + leave_t * jnp.einsum(
        "csn,hcpn->cshp", b_blocks, grads_bf, preferred_element_type=jnp.float32
    )
    x_grad = step_t * w_grad + d_skip[:, None] * dy_float
    step_grad = jnp.sum(x_float * w_grad, axis=3).transpose(2, 0, 1).reshape(head_count, length)
    mixing = jnp.einsum("cthp,cshp->hcts", dy_bf, w_blocks, preferred_element_type=jnp.float32)
    mixed_sum = jnp.sum(mixing * decay_pair, axis=0).astype(jnp.bfloat16)
    c_grad = jnp.einsum(
        "cts,csn->ctn", mixed_sum, b_blocks, preferred_element_type=jnp.float32
    ) + jnp.sum(
        enter_t
        * jnp.einsum("cthp,hcpn->cthn", dy_bf, states_bf, preferred_element_type=jnp.float32),
        axis=2,
    )
    b_grad = jnp.einsum(
        "cts,ctn->csn", mixed_sum, c_blocks, preferred_element_type=jnp.float32
    ) + jnp.sum(
        leave_t
        * jnp.einsum("cshp,hcpn->cshn", w_blocks, grads_bf, preferred_element_type=jnp.float32),
        axis=2,
    )
    partial_value = jnp.concatenate([b_grad, c_grad], axis=-1).reshape(length, 2 * state_dim)
    own_rows = length // lax.axis_size(HEAD)
    first_row = lax.axis_index(HEAD) * own_rows
    own_grad = sum_at_owner(partial_value.astype(jnp.bfloat16), HEAD, 0)
    own_pre = lax.dynamic_slice_in_dim(bc_pre, first_row, own_rows, 0)
    own_slope = own_grad * silu_slope(own_pre)
    next_rim = from_behind(own_slope[: conv_len - 1], SEQ_HEAD, -1)
    bc_raw_grad = conv_adjoint(jnp.concatenate([own_slope, next_rim], axis=0), conv_bc, own_rows)
    own_raw = lax.dynamic_slice_in_dim(bc_extended, first_row, own_rows + conv_len - 1, 0)
    conv_bc_part = conv_weight_grad(own_slope, own_raw, conv_len)
    x_slope = x_grad.reshape(length, channels) * silu_slope(x_pre)
    x_next_rim = from_behind(x_slope[: conv_len - 1], SEQ, -1)
    x_raw_grad = conv_adjoint(
        jnp.concatenate([x_slope, x_next_rim], axis=0), conv_x, length
    ).astype(jnp.bfloat16)
    conv_x_part = conv_weight_grad(x_slope, x_extended, conv_len)
    conv_x_grad = over_copies(conv_x_part, SEQ)
    conv_bc_grad = by_axis(conv_bc_part, SEQ_HEAD)
    return (x_raw_grad, gate_grad, step_grad, bc_raw_grad, conv_x_grad, conv_bc_grad)


def solution(mesh):
    torus = Mesh(
        mesh.devices.reshape(4, 2, 8, 2, 2), ("seq_0", "seq_1", "head_0", "head_1", "head_2")
    )
    placed = (
        P(SEQ, HEAD),
        P(SEQ, HEAD),
        P(SEQ, None),
        P(HEAD, SEQ),
        P(HEAD),
        P(HEAD),
        P(None, HEAD),
        P(),
        P(SEQ, HEAD),
    )
    return jax.shard_map(
        local,
        mesh=torus,
        in_specs=placed,
        out_specs=(P(SEQ, HEAD), P(SEQ, HEAD), P(HEAD, SEQ), P(SEQ_HEAD, None), P(None, HEAD), P()),
        check_vma=False,
    )
```

profile of v0, /device:TPU:1, one launch (start us, length us, event | category | flops | bytes accessed | tf_op | source)
XLA Modules:
  0.0 175.0 jit_solution(4385628365003967159)
XLA Ops:
  2.0 5.6 %collective-permute-start = (bf16[3,512]{1,0:T(4,128)(2,1)S(1)}, bf16[3,512]{1,0:T(4,128)(2,1)S(1)}, u32[]{:S(2)}, u32[]{:S(2)}) collective-permute-start(bf16[3,512]{1,0:T(4,128)(2,1)S(1)} %pad_maximum_fusion.4), channel_id=1, source_target_pairs={{0,32},{32,64},{64,96},{96,128},{128,160},{160,192},{192,224},{1,3... | collective-permute-start | bytes 9224 | tf_op jit(solution)/shard_map/ppermute | solution.py:18
  9.1 4.8 %reduce-window.6 = f32[4,4,2,128]{3,2,1,0:T(2,128)S(1)} reduce-window(f32[4,4,2,128]{3,2,1,0:T(2,128)S(1)} %broadcast_multiply_fusion, f32[]{:T(128)} %constant.17.clone.1), window={size=1x1x1x128 pad=0_0x0_0x0_0x127_0}, to_apply=%region_0.1 | reduce-window | flops 520192 | bytes 32772 | tf_op jit(solution)/shard_map/reduce-window
  15.2 4.4 %all-to-all-start.1 = ((bf16[8,1,4]{2,1,0:T(2,128)(2,1)}), bf16[8,1,4]{2,1,0:T(2,128)(2,1)S(1)}, u32[]{:S(2)}, u32[]{:S(2)}) async-start(bf16[8,1,4]{2,1,0:T(2,128)(2,1)} %broadcast_in_dim.48), calls=%async_computation.1 | async-start | bytes 8192 | tf_op jit(solution)/shard_map/all_to_all | solution.py:23
  21.5 0.8 fusion.105
  22.3 0.8 fusion.106
  23.3 2.0 %reshape.244 = f32[4,256,4,64]{3,2,1,0:T(4,128)S(1)} reshape(bf16[1024,256]{1,0:T(8,128)(2,1)} %param.10) | data formatting | bytes 1572864 | tf_op jit(solution)/shard_map/convert_element_type | solution.py:159
  25.3 0.8 copy.210
  26.1 2.3 %reshape.243 = f32[4,256,4,64]{3,2,1,0:T(4,128)S(1)} reshape(bf16[1024,256]{1,0:T(8,128)(2,1)} %param.17) | data formatting | bytes 1572864 | tf_op jit(solution)/shard_map/convert_element_type | solution.py:160
  28.4 1.6 copy.211
  30.1 2.5 %fusion.22 = (bf16[4,256,4,64]{1,3,2,0:T(8,128)(2,1)S(1)}, bf16[4,256,4,64]{1,3,2,0:T(8,128)(2,1)}) fusion(f32[4,256,4]{1,2,0:T(4,128)S(1)} %get-tuple-element.65, f32[4,256,4,64]{1,3,2,0:T(8,128)} %copy.211, f32[4,256,4,64]{1,3,2,0:T(8,128)S(1)} %copy.210), kind=kLoop, calls=%fused_computation.45 | loop fusion | flops 2359296 | bytes 3162112 | tf_op jit(solution)/shard_map/convert_element_type | solution.py:163
  37.6 2.3 %multiply_convert_fusion.4 = (bf16[1024,256]{1,0:T(8,128)(2,1)S(1)}, f32[1024,256]{1,0:T(8,128)}, f32[1024,256]{1,0:T(8,128)S(1)}) fusion(f32[256]{0:T(256)S(1)} %bitcast.155, f32[256]{0:T(256)S(1)} %bitcast.157, bf16[1024,256]{1,0:T(8,128)(2,1)S(1)} %copy-done.5, bf16[3,256]{1,0:T(4,128)(2,1)S(1)} %get-tuple-element.74, f32[256]{0:T(256)S(1)} %bitcast.153, ...), kind=kLoop, calls=%fused_computation.73 | loop fusion | flops 13369344 | bytes 3681280 | tf_op jit(solution)/shard_map/convert_element_type | solution.py:138
  41.1 1.2 fusion.51
  42.4 0.9 broadcast_in_dim.45
  43.3 6.6 %all-to-all-start = ((bf16[8,4,64,128]{3,2,1,0:T(8,128)(2,1)}), bf16[8,4,64,128]{3,2,1,0:T(8,128)(2,1)}, u32[]{:S(2)}, u32[]{:S(2)}) async-start(bf16[8,4,64,128]{3,2,1,0:T(8,128)(2,1)} %broadcast_in_dim.45), calls=%async_computation | async-start | bytes 1048576 | tf_op jit(solution)/shard_map/all_to_all | solution.py:23
  49.9 1.3 fusion.108
  51.2 0.9 reshape.245
  52.1 0.8 copy.227
  52.9 0.8 fusion.71
  53.8 2.6 %fusion.6 = f32[4,256,4,64]{1,3,2,0:T(8,128)S(1)} fusion(bf16[4,256,4,64]{1,3,2,0:T(8,128)(2,1)} %get-tuple-element.51, f32[256,256]{1,0:T(8,128)} %fusion.56, f32[4,4,256]{2,1,0:T(4,128)S(1)} %reduce_window_sum.37, f32[4,256,256]{2,1,0:T(8,128)} %fusion.108), kind=kOutput, calls=%fused_computation.13 | convolution fusion | flops 139460608 | bytes 2899968 | tf_op jit(solution)/shard_map/hcts,cthp->cshp/dot_general | solution.py:202
  56.4 2.3 %all-to-all-done = bf16[8,4,64,128]{3,2,1,0:T(8,128)(2,1)} async-done(((bf16[8,4,64,128]{3,2,1,0:T(8,128)(2,1)}), bf16[8,4,64,128]{3,2,1,0:T(8,128)(2,1)}, u32[]{:S(2)}, u32[]{:S(2)}) %all-to-all-start) | async-done | bytes 524320 | tf_op jit(solution)/shard_map/all_to_all | solution.py:23
  58.7 1.2 convert_select_fusion.1
  61.0 1.3 fusion.20
  62.3 2.2 %multiply_reduce_fusion.1 = (f32[4,256,4]{1,2,0:T(4,128)}, f32[4,256,4,64]{1,3,2,0:T(8,128)}, bf16[4,256,4,64]{1,3,2,0:T(8,128)(2,1)S(1)}, bf16[4,256,4,64]{1,3,2,0:T(8,128)(2,1)S(1)}) fusion(f32[4,256,4,64]{1,3,2,0:T(8,128)S(1)} %copy.227, bf16[4,256,4,64]{1,3,2,0:T(8,128)(2,1)S(1)} %copy-done.10, f32[4]{0:T(128)S(1)} %copy-done.26, ...), kind=kOutput, calls=%fused_computation.65 | convolution fusion | flops 70512640 | bytes 5292048 | tf_op jit(solution)/shard_map/csn,hcpn->cshp/dot_general | solution.py:204
  64.5 2.4 %multiply_reduce_fusion = bf16[4,256,256]{2,1,0:T(8,128)(2,1)} fusion(f32[256,256]{1,0:T(8,128)S(1)} %copy-done.16, f32[4,4,256]{2,1,0:T(4,128)S(1)} %reduce_window_sum.37, bf16[4,256,4,64]{1,3,2,0:T(8,128)(2,1)S(1)} %get-tuple-element.57, bf16[4,256,4,64]{1,3,2,0:T(8,128)(2,1)S(1)} %copy-done.10), kind=kOutput, calls=%fused_computation | convolution fusion | flops 139198464 | bytes 1851392 | tf_op jit(solution)/shard_map/cthp,cshp->hcts/dot_general | solution.py:209
  67.2 1.3 fusion.48
  68.5 0.9 broadcast_in_dim.51
  69.4 5.2 %all-to-all-start.2 = ((bf16[8,4,64,128]{3,2,1,0:T(8,128)(2,1)}), bf16[8,4,64,128]{3,2,1,0:T(8,128)(2,1)}, u32[]{:S(2)}, u32[]{:S(2)}) async-start(bf16[8,4,64,128]{3,2,1,0:T(8,128)(2,1)} %broadcast_in_dim.51), calls=%async_computation.2 | async-start | bytes 1048576 | tf_op jit(solution)/shard_map/all_to_all | solution.py:23
  74.6 1.8 %copy.257 = f32[4,256,4,64]{3,2,1,0:T(4,128)S(1)} copy(f32[4,256,4,64]{1,3,2,0:T(8,128)} %get-tuple-element.55) | data formatting | bytes 2097152 | tf_op jit(solution)/shard_map/reshape | solution.py:235
  76.5 2.2 %reshape.241 = f32[1024,256]{1,0:T(8,128)} reshape(f32[4,256,4,64]{3,2,1,0:T(4,128)S(1)} %copy.257) | data formatting | bytes 2097152 | tf_op jit(solution)/shard_map/reshape | solution.py:235
  78.6 3.5 %fusion.28 = (f32[256]{0:T(256)S(1)}, f32[256]{0:T(256)S(1)}, f32[256]{0:T(256)S(1)}, f32[256]{0:T(256)S(1)}, f32[1024,256]{1,0:T(8,128)S(1)}) fusion(bf16[1024,256]{1,0:T(8,128)(2,1)} %param.9, bf16[3,256]{1,0:T(4,128)(2,1)S(1)} %get-tuple-element.75, f32[1024,256]{1,0:T(8,128)} %reshape.241, f32[256]{0:T(256)S(1)} %bitcast.146, f32[256]{0:T(256)S(1)} %bitcast.149, ...), kind=kLoop, calls=%fused_computation.51 | loop fusion | flops 11533312 | bytes 2631168 | tf_op jit(solution)/shard_map/reduce_sum | solution.py:105
  82.8 1.3 collective-permute-start.1
  85.5 7.8 %all-to-all-start.4 = ((f32[8,4,256]{2,1,0:T(4,128)}), f32[8,4,256]{2,1,0:T(4,128)S(1)}, u32[]{:S(2)}, u32[]{:S(2)}) async-start(f32[8,4,256]{2,1,0:T(4,128)} %broadcast_in_dim.53), calls=%async_computation.4 | async-start | bytes 65536 | tf_op jit(solution)/shard_map/all_to_all | solution.py:23
  93.3 1.2 convert_select_fusion
  96.1 1.3 fusion.21
  98.3 1.0 copy.244
  99.9 13.9 %all-to-all-start.3 = ((bf16[32,32,256]{2,1,0:T(8,128)(2,1)}), bf16[32,32,256]{2,1,0:T(8,128)(2,1)}, u32[]{:S(2)}, u32[]{:S(2)}) async-start(bf16[32,32,256]{2,1,0:T(8,128)(2,1)} %bitcast.50), calls=%async_computation.3 | async-start | bytes 1048576 | tf_op jit(solution)/shard_map/all_to_all | solution.py:61
  113.8 3.7 %fusion.9 = f32[4,256,4,64]{1,3,2,0:T(8,128)} fusion(bf16[4,256,4,64]{1,3,2,0:T(8,128)(2,1)} %copy-done.12, f32[256,256]{1,0:T(8,128)} %fusion.56, f32[4,4,256]{2,1,0:T(4,128)S(1)} %reduce_window_sum.37, f32[4,256,256]{2,1,0:T(8,128)} %fusion.108), kind=kOutput, calls=%fused_computation.14 | convolution fusion | flops 139460608 | bytes 2899968 | tf_op jit(solution)/shard_map/hcts,cshp->cthp/dot_general | solution.py:193
  117.6 2.0 %fusion.35 = bf16[1024,256]{1,0:T(8,128)(2,1)} fusion(f32[3,256]{1,0:T(4,128)} %collective-permute-done.1, f32[1024,256]{1,0:T(8,128)S(1)} %get-tuple-element.45, f32[256]{0:T(256)S(1)} %bitcast.147, f32[256]{0:T(256)S(1)} %bitcast.150, f32[256]{0:T(256)S(1)} %bitcast.144, f32[256]{0:T(256)S(1)} %bitcast.141), kind=kLoop, calls=%fused_computation.58 | loop fusion | flops 2883584 | bytes 1580032 | tf_op jit(solution)/shard_map/convert_element_type | solution.py:239
  120.2 2.5 %fusion.17 = bf16[4,256,4,64]{1,3,2,0:T(8,128)(2,1)S(1)} fusion(f32[4,256,4,64]{1,3,2,0:T(8,128)} %copy.211, f32[4,256,4,64]{1,3,2,0:T(8,128)} %fusion.9, bf16[4,256,128,1]{2,1,3,0:T(8,128)(2,1)S(1)} %bitcast.126, f32[4,256,4,64]{1,3,2,0:T(8,128)S(1)} %copy-done.1, f32[4,256,4,64]{1,3,2,0:T(8,128)} %copy-done.2, f32[4]{0:T(128)S(1)} %copy-done.27, ...), kind=kOutput, calls=%fused_computation.32 | convolution fusion | flops 70778880 | bytes 5259280 | tf_op jit(solution)/shard_map/ctn,hcpn->cthp/dot_general | solution.py:195
  123.4 1.5 reshape.242
  124.8 5.6 %all-to-all-done.3 = bf16[32,32,256]{2,1,0:T(8,128)(2,1)} async-done(((bf16[32,32,256]{2,1,0:T(8,128)(2,1)}), bf16[32,32,256]{2,1,0:T(8,128)(2,1)}, u32[]{:S(2)}, u32[]{:S(2)}) %all-to-all-start.3) | async-done | bytes 524320 | tf_op jit(solution)/shard_map/all_to_all | solution.py:61
  130.4 1.1 convert_reduce_fusion
  132.4 7.2 %psum.35 = f32[4,256]{1,0:T(4,128)S(1)} all-reduce(f32[4,256]{1,0:T(4,128)S(1)} %pad_maximum_fusion.6), channel_id=1, replica_groups=mesh['seq_0'=4,'seq_1'=2,'head_0'=8,'head_1'=2,'head_2'=2] {'seq_0'}, use_global_device_ids=true, to_apply=%region_18.19 | all-reduce | flops 1024 | bytes 8192 | tf_op jit(solution)/shard_map/psum | solution.py:71
  139.6 5.6 %psum.36 = f32[4,256]{1,0:T(4,128)S(1)} all-reduce(f32[4,256]{1,0:T(4,128)S(1)} %psum.35), channel_id=1, replica_groups=mesh['seq_0'=4,'seq_1'=2,'head_0'=8,'head_1'=2,'head_2'=2] {'seq_1'}, use_global_device_ids=true, to_apply=%region_19.20 | all-reduce | flops 1024 | bytes 8192 | tf_op jit(solution)/shard_map/psum | solution.py:71
  145.2 11.9 %psum.37 = f32[4,256]{1,0:T(4,128)S(1)} all-reduce(f32[4,256]{1,0:T(4,128)S(1)} %psum.36), channel_id=1, replica_groups=mesh['seq_0'=4,'seq_1'=2,'head_0'=8,'head_1'=2,'head_2'=2] {'head_0'}, use_global_device_ids=true, to_apply=%region_20.21 | all-reduce | flops 1024 | bytes 8192 | tf_op jit(solution)/shard_map/psum | solution.py:71
  157.1 4.1 %psum.38 = f32[4,256]{1,0:T(4,128)S(1)} all-reduce(f32[4,256]{1,0:T(4,128)S(1)} %psum.37), channel_id=1, replica_groups=mesh['seq_0'=4,'seq_1'=2,'head_0'=8,'head_1'=2,'head_2'=2] {'head_1'}, use_global_device_ids=true, to_apply=%region_21.22 | all-reduce | flops 1024 | bytes 8192 | tf_op jit(solution)/shard_map/psum | solution.py:71
  161.2 10.1 %collective-permute-start.2 = (f32[3,256]{1,0:T(4,128)S(1)}, f32[3,256]{1,0:T(4,128)S(1)}, u32[]{:S(2)}, u32[]{:S(2)}) collective-permute-start(f32[3,256]{1,0:T(4,128)S(1)} %slice.287), channel_id=1, source_target_pairs={{1,0},{2,1},{3,2},{4,3},{5,4},{6,5},{7,6},{8,7},{9,8},{10,9},{11,1... | collective-permute-start | bytes 9224 | tf_op jit(solution)/shard_map/ppermute | solution.py:18
  171.3 3.1 %psum.39 = f32[4,256]{1,0:T(4,128)} all-reduce(f32[4,256]{1,0:T(4,128)S(1)} %psum.38), channel_id=1, replica_groups=mesh['seq_0'=4,'seq_1'=2,'head_0'=8,'head_1'=2,'head_2'=2] {'head_2'}, use_global_device_ids=true, to_apply=%region_22.23 | all-reduce | flops 1024 | bytes 8192 | tf_op jit(solution)/shard_map/psum | solution.py:71
  (138 shorter events, 21.2 us)
Async XLA Ops:
  2.0 35.6 %collective-permute-start = (bf16[3,512]{1,0:T(4,128)(2,1)S(1)}, bf16[3,512]{1,0:T(4,128)(2,1)S(1)}, u32[]{:S(2)}, u32[]{:S(2)}) collective-permute-start(bf16[3,512]{1,0:T(4,128)(2,1)S(1)} %pad_maximum_fusion.4), channel_id=1, source_target_pairs={{0,32},{32,64},{64,96},{96,128},{128,160},{160,192},{192,224},{1,3... | collective-permute-start | bytes 9224 | tf_op jit(solution)/shard_map/ppermute | solution.py:18
  15.2 17.4 %all-to-all-start.1 = ((bf16[8,1,4]{2,1,0:T(2,128)(2,1)}), bf16[8,1,4]{2,1,0:T(2,128)(2,1)S(1)}, u32[]{:S(2)}, u32[]{:S(2)}) async-start(bf16[8,1,4]{2,1,0:T(2,128)(2,1)} %broadcast_in_dim.48), calls=%async_computation.1 | async-start | bytes 8192 | tf_op jit(solution)/shard_map/all_to_all | solution.py:23
  19.7 13.0 %copy-start.21 = (pred[8]{0:T(512)(128)(4,1)}, pred[8]{0:T(512)(128)(4,1)S(1)}, u32[]{:S(2)}) copy-start(pred[8]{0:T(512)(128)(4,1)S(1)} %iota_compare_fusion.3) | copy-start | bytes 28
  19.7 13.0 %copy-start.22 = (pred[8]{0:T(512)(128)(4,1)}, pred[8]{0:T(512)(128)(4,1)S(1)}, u32[]{:S(2)}) copy-start(pred[8]{0:T(512)(128)(4,1)S(1)} %iota_compare_fusion.4) | copy-start | bytes 28
  26.1 3.9 %copy-start = (f32[4,256,4,64]{1,3,2,0:T(8,128)}, f32[4,256,4,64]{1,3,2,0:T(8,128)S(1)}, u32[]{:S(2)}) copy-start(f32[4,256,4,64]{1,3,2,0:T(8,128)S(1)} %copy.210) | copy-start | bytes 3145732
  30.1 7.6 %copy-start.5 = (bf16[1024,256]{1,0:T(8,128)(2,1)S(1)}, bf16[1024,256]{1,0:T(8,128)(2,1)}, u32[]{:S(2)}) copy-start(bf16[1024,256]{1,0:T(8,128)(2,1)} %param.11) | copy-start | bytes 1572868
  30.1 7.6 %copy-start.6 = (bf16[1024,256]{1,0:T(8,128)(2,1)S(1)}, bf16[1024,256]{1,0:T(8,128)(2,1)}, u32[]{:S(2)}) copy-start(bf16[1024,256]{1,0:T(8,128)(2,1)} %param.9) | copy-start | bytes 1572868
  40.0 11.2 %copy-start.3 = (bf16[1024,128]{1,0:T(8,128)(2,1)}, bf16[1024,128]{1,0:T(8,128)(2,1)S(1)}, u32[]{:S(2)}) copy-start(bf16[1024,128]{1,0:T(8,128)(2,1)S(1)} %get-tuple-element.61) | copy-start | bytes 786436
  40.3 0.8 copy-start.8
  43.3 15.4 %all-to-all-start = ((bf16[8,4,64,128]{3,2,1,0:T(8,128)(2,1)}), bf16[8,4,64,128]{3,2,1,0:T(8,128)(2,1)}, u32[]{:S(2)}, u32[]{:S(2)}) async-start(bf16[8,4,64,128]{3,2,1,0:T(8,128)(2,1)} %broadcast_in_dim.45), calls=%async_computation | async-start | bytes 1048576 | tf_op jit(solution)/shard_map/all_to_all | solution.py:23
  52.9 9.3 %copy-start.2 = (f32[4,256,4,64]{1,3,2,0:T(8,128)}, f32[4,256,4,64]{1,3,2,0:T(8,128)S(1)}, u32[]{:S(2)}) copy-start(f32[4,256,4,64]{1,3,2,0:T(8,128)S(1)} %copy.227) | copy-start | bytes 3145732
  53.8 4.9 %copy-start.23 = (pred[8]{0:T(512)(128)(4,1)S(1)}, pred[8]{0:T(512)(128)(4,1)}, u32[]{:S(2)}) copy-start(pred[8]{0:T(512)(128)(4,1)} %copy-done.22) | copy-start | bytes 28
  56.4 3.7 %copy-start.19 = (f32[4,4]{1,0:T(4,128)S(1)}, f32[4,4]{1,0:T(4,128)}, u32[]{:S(2)}) copy-start(f32[4,4]{1,0:T(4,128)} %copy.221) | copy-start | bytes 196
  59.9 0.7 copy-start.20
  59.9 0.8 copy-start.24
  59.9 1.0 copy-start.9
  59.9 1.0 copy-start.25
  60.0 2.2 %copy-start.10 = (bf16[4,256,4,64]{1,3,2,0:T(8,128)(2,1)S(1)}, bf16[4,256,4,64]{1,3,2,0:T(8,128)(2,1)}, u32[]{:S(2)}) copy-start(bf16[4,256,4,64]{1,3,2,0:T(8,128)(2,1)} %get-tuple-element.51) | copy-start | bytes 1572868
  60.1 2.2 %copy-start.17 = (f32[4,1024]{1,0:T(4,128)S(1)}, f32[4,1024]{1,0:T(4,128)}, u32[]{:S(2)}) copy-start(f32[4,1024]{1,0:T(4,128)} %param.12) | copy-start | bytes 49156
  60.1 2.2 %copy-start.26 = (f32[4]{0:T(128)S(1)}, f32[4]{0:T(128)}, u32[]{:S(2)}) copy-start(f32[4]{0:T(128)} %param.14) | copy-start | bytes 52
  62.3 2.2 %copy-start.16 = (f32[256,256]{1,0:T(8,128)S(1)}, f32[256,256]{1,0:T(8,128)}, u32[]{:S(2)}) copy-start(f32[256,256]{1,0:T(8,128)} %fusion.56) | copy-start | bytes 786436
  64.5 2.4 %copy-start.12 = (bf16[4,256,4,64]{1,3,2,0:T(8,128)(2,1)}, bf16[4,256,4,64]{1,3,2,0:T(8,128)(2,1)S(1)}, u32[]{:S(2)}) copy-start(bf16[4,256,4,64]{1,3,2,0:T(8,128)(2,1)S(1)} %get-tuple-element.57) | copy-start | bytes 1572868
  69.4 15.5 %all-to-all-start.2 = ((bf16[8,4,64,128]{3,2,1,0:T(8,128)(2,1)}), bf16[8,4,64,128]{3,2,1,0:T(8,128)(2,1)}, u32[]{:S(2)}, u32[]{:S(2)}) async-start(bf16[8,4,64,128]{3,2,1,0:T(8,128)(2,1)} %broadcast_in_dim.51), calls=%async_computation.2 | async-start | bytes 1048576 | tf_op jit(solution)/shard_map/all_to_all | solution.py:23
  78.6 5.5 %copy-start.13 = (bf16[4,256,4,64]{1,3,2,0:T(8,128)(2,1)S(1)}, bf16[4,256,4,64]{1,3,2,0:T(8,128)(2,1)}, u32[]{:S(2)}) copy-start(bf16[4,256,4,64]{1,3,2,0:T(8,128)(2,1)} %copy-done.12) | copy-start | bytes 1572868
  78.6 6.0 %copy-start.4 = (bf16[1024,128]{1,0:T(8,128)(2,1)S(1)}, bf16[1024,128]{1,0:T(8,128)(2,1)}, u32[]{:S(2)}) copy-start(bf16[1024,128]{1,0:T(8,128)(2,1)} %copy-done.3) | copy-start | bytes 786436
  78.6 6.0 %copy-start.7 = (bf16[4,256,256]{2,1,0:T(8,128)(2,1)S(1)}, bf16[4,256,256]{2,1,0:T(8,128)(2,1)}, u32[]{:S(2)}) copy-start(bf16[4,256,256]{2,1,0:T(8,128)(2,1)} %multiply_reduce_fusion) | copy-start | bytes 1572868
  82.8 34.8 %collective-permute-start.1 = (f32[3,256]{1,0:T(4,128)}, f32[3,256]{1,0:T(4,128)}, u32[]{:S(2)}, u32[]{:S(2)}) collective-permute-start(f32[3,256]{1,0:T(4,128)} %slice.280), channel_id=1, source_target_pairs={{32,0},{64,32},{96,64},{128,96},{160,128},{192,160},{224,192},{33,... | collective-permute-start | bytes 9224 | tf_op jit(solution)/shard_map/ppermute | solution.py:18
  84.1 10.5 %copy-start.18 = (f32[4,4]{1,0:T(4,128)S(1)}, f32[4,4]{1,0:T(4,128)}, u32[]{:S(2)}) copy-start(f32[4,4]{1,0:T(4,128)} %copy.230) | copy-start | bytes 196
  85.5 14.4 %all-to-all-start.4 = ((f32[8,4,256]{2,1,0:T(4,128)}), f32[8,4,256]{2,1,0:T(4,128)S(1)}, u32[]{:S(2)}, u32[]{:S(2)}) async-start(f32[8,4,256]{2,1,0:T(4,128)} %broadcast_in_dim.53), calls=%async_computation.4 | async-start | bytes 65536 | tf_op jit(solution)/shard_map/all_to_all | solution.py:23
  94.6 2.8 %copy-start.11 = (bf16[4,256,4,64]{1,3,2,0:T(8,128)(2,1)S(1)}, bf16[4,256,4,64]{1,3,2,0:T(8,128)(2,1)}, u32[]{:S(2)}) copy-start(bf16[4,256,4,64]{1,3,2,0:T(8,128)(2,1)} %get-tuple-element.51) | copy-start | bytes 1572868
  97.4 0.8 copy-start.14
  99.9 30.5 %all-to-all-start.3 = ((bf16[32,32,256]{2,1,0:T(8,128)(2,1)}), bf16[32,32,256]{2,1,0:T(8,128)(2,1)}, u32[]{:S(2)}, u32[]{:S(2)}) async-start(bf16[32,32,256]{2,1,0:T(8,128)(2,1)} %bitcast.50), calls=%async_computation.3 | async-start | bytes 1048576 | tf_op jit(solution)/shard_map/all_to_all | solution.py:61
  113.8 6.4 %copy-start.1 = (f32[4,256,4,64]{1,3,2,0:T(8,128)S(1)}, f32[4,256,4,64]{1,3,2,0:T(8,128)}, u32[]{:S(2)}) copy-start(f32[4,256,4,64]{1,3,2,0:T(8,128)} %copy-done) | copy-start | bytes 3145732
  113.8 6.4 %copy-start.15 = (bf16[4,4,64,128]{3,1,2,0:T(4,128)(2,1)S(1)}, bf16[4,4,64,128]{3,1,2,0:T(4,128)(2,1)}, u32[]{:S(2)}) copy-start(bf16[4,4,64,128]{3,1,2,0:T(4,128)(2,1)} %copy-done.14) | copy-start | bytes 786436
  113.8 6.4 %copy-start.27 = (f32[4]{0:T(128)S(1)}, f32[4]{0:T(128)}, u32[]{:S(2)}) copy-start(f32[4]{0:T(128)} %param.14) | copy-start | bytes 52
  161.2 13.2 %collective-permute-start.2 = (f32[3,256]{1,0:T(4,128)S(1)}, f32[3,256]{1,0:T(4,128)S(1)}, u32[]{:S(2)}, u32[]{:S(2)}) collective-permute-start(f32[3,256]{1,0:T(4,128)S(1)} %slice.287), channel_id=1, source_target_pairs={{1,0},{2,1},{3,2},{4,3},{5,4},{6,5},{7,6},{8,7},{9,8},{10,9},{11,1... | collective-permute-start | bytes 9224 | tf_op jit(solution)/shard_map/ppermute | solution.py:18
where the time goes:
time: 176 us; the launch traced here: 175 us
  starting transfers between devices  55 us (31%)
  blocking collectives  31.9 us (18%)
  local copies, waits for them, and re-layouts  30.3 us (17%)
  other arithmetic  26.2 us (15%)
  matrix products  21.9 us (12%)
  waiting for transfers between devices  8.42 us (5%)
    psum x5, blocking collectives, by_axis(): x = lax.psum(x, axis)  31.9 us
    all_to_all x4, starting transfers between devices, sent_to_all(): lax.all_to_all(jnp.broadcast_to(x[None], (length, *x.shape)), axis, 0, 0,...  24.1 us
    ppermute x3, starting transfers between devices, from_behind(): lax.ppermute(value, axis, [(source, source + steps) for source in range(i...  17.1 us
    all_to_all x1, starting transfers between devices, sum_at_owner(): tiles = lax.all_to_all(in_blocks(x, dim, length), axis, 0, 0, tiled=True)  13.9 us
    all_to_all x1, waiting for transfers between devices, sum_at_owner(): tiles = lax.all_to_all(in_blocks(x, dim, length), axis, 0, 0, tiled=True)  5.56 us
    slice x17, local copies, waits for them, and re-layouts, combined_pairwise(): part[side::2]  4.98 us
    another operation x3, other arithmetic  4.91 us
    reduce_sum x2, other arithmetic, conv_weight_grad(): jnp.sum(slope_rows * raw_extended[start_row:start_row + length].astype(jn...  4.35 us
  transfers between devices with their start and end apart: 8, of which 3 were waited for; matrix products, arithmetic and copies ran while one was open for 33% of the time, Pallas kernels for 0%

commit v1 on v0

v1 whole, which is shorter than its diff:
```python
import functools

import jax
import jax.numpy as jnp
from jax import lax
from jax.experimental import pallas as pl
from jax.experimental.pallas import tpu as pltpu
from jax.sharding import Mesh
from jax.sharding import PartitionSpec as P

HEAD_DIM = 64
BLOCK = 256
TAPS = 4
SEQ = ("seq_0", "seq_1")
HEAD = ("head_0", "head_1", "head_2")
SEQ_HEAD = SEQ + HEAD
F32, BF16 = jnp.float32, jnp.bfloat16


def mm(a, b, dims=((1,), (0,))):
    return lax.dot_general(a, b, (dims, ((), ())), preferred_element_type=F32)


NT = ((1,), (1,))
TN = ((0,), (0,))


def parts3(v):
    p1 = v.astype(BF16)
    r1 = v - p1.astype(F32)
    p2 = r1.astype(BF16)
    r2 = r1 - p2.astype(F32)
    return p1, p2, r2.astype(BF16)


def sigmoid(v):
    return 1.0 / (1.0 + jnp.exp(-v))


def by_head(scalars, lanes):
    out = jnp.full(lanes.shape, scalars[3], F32)
    for h in (2, 1, 0):
        out = jnp.where(lanes == h, scalars[h], out)
    return out


def kernel(
    dims, T, W,
    xraw, zg, bcr, dt, a_s, d_s, cvx, cvb, dout,
    xg_o, gg_o, sg_o, bg_o, cx_o, cb_o,
    XF, BCF, XS, BCS, GZ, DTE, ENT, LEA, YIN, WGIN, XSL, BS,
    XP, WX, WL, DY, DYE, BCP, MX,
    GC, DC, WP, TOT, EK, BK, LS, NS, SB, GB, EB, SLOT,
    KH, WXM, DYM, HXR, HBR, HSX, HSB,
    PR, RA, A1S, A1K, RB, A2, ZS, RZ, CXS, CBS, CBL, CBT, CBZ,
    s_h, r_h, s_st, r_st, s_sl, r_sl, s_a, r_a, s_b, r_b, s_z, r_z,
    s_cx, r_cx, s_cb, r_cb, s_cc, r_cc, s_cz, r_cz,
):
    nx, nyh, nz, nyl, nc = dims
    nseq = nx * nyh
    nb = T // BLOCK
    heads = W // HEAD_DIM
    own = T // (nz * nyl * nc)
    sx, sy = lax.axis_index("seq_0"), lax.axis_index("seq_1")
    s = sx * nyh + sy
    z, yl, c = (lax.axis_index(n) for n in HEAD)

    def at_seq(p):
        return {"seq_0": p // nyh, "seq_1": lax.rem(p, nyh)}

    def other(d):
        wrapped = (s + d) // nseq
        return s + d - nseq * wrapped, wrapped

    def other_z(d):
        return lax.rem(z + d, nz)

    def send(src, dst, ss, rs, dev):
        return pltpu.make_async_remote_copy(
            src_ref=src, dst_ref=dst, send_sem=ss, recv_sem=rs,
            device_id=dev, device_id_type=pl.DeviceIdType.MESH,
        )

    core_dev = {"head_2": 1 - c}
    y_dev = {"head_1": 1 - yl}

    barrier = pltpu.get_barrier_semaphore()

    def greet(dev):
        pl.semaphore_signal(barrier, inc=1, device_id=dev, device_id_type=pl.DeviceIdType.MESH)

    for d in range(1, nseq):
        greet(at_seq(other(d)[0]))
    for d in range(1, nz):
        greet({"head_0": other_z(d)})
    greet(core_dev)
    greet(y_dev)

    rows16 = lax.broadcasted_iota(jnp.int32, (heads, BLOCK), 0)
    a_col = by_head([a_s[h] for h in range(heads)], rows16)
    for k in range(nb):
        piece = dt[:, k * BLOCK : (k + 1) * BLOCK]
        DC[k * heads : (k + 1) * heads, :] = piece
        GC[k * heads : (k + 1) * heads, :] = piece * a_col
    n16 = nb * heads
    ri = lax.broadcasted_iota(jnp.int32, (BLOCK, BLOCK), 0)
    ci = lax.broadcasted_iota(jnp.int32, (BLOCK, BLOCK), 1)
    tri = (ri <= ci).astype(F32).astype(BF16)
    w3 = mm(jnp.concatenate(parts3(GC[...]), axis=0), tri)
    within = w3[:n16] + w3[n16 : 2 * n16] + w3[2 * n16 :]
    GC[...] = within
    wp = jnp.concatenate(parts3(within), axis=0)
    dp = jnp.concatenate(parts3(DC[...]), axis=0)
    WP[...] = wp
    rr = lax.rem(lax.broadcasted_iota(jnp.int32, (3 * n16, W), 0), n16)
    ll = lax.broadcasted_iota(jnp.int32, (3 * n16, W), 1) // HEAD_DIM

    def blk(k, n=BLOCK):
        return pl.ds(pl.multiple_of(k * n, n), n)

    def expand(k, carry):
        hot = ((rr // heads == k) & (lax.rem(rr, heads) == ll)).astype(F32).astype(BF16)
        wexp = mm(wp, hot, TN)
        total = wexp[BLOCK - 1 : BLOCK, :]
        TOT[k] = jnp.broadcast_to(total, (8, W))
        ENT[blk(k), :] = jnp.exp(-wexp)
        LEA[blk(k), :] = jnp.exp(jnp.minimum(wexp - total, 0.0))
        DTE[blk(k), :] = mm(dp, hot, TN)
        return carry

    lax.fori_loop(0, nb, expand, 0)

    CH = 64

    def gates(i, carry):
        r = blk(i, CH)
        zv = zg[r, :].astype(F32)
        q = sigmoid(zv)
        up = dout[r, :].astype(F32)
        dy = (up * (zv * q)).astype(BF16)
        DY[r, :] = dy
        GZ[r, :] = up * (q * (1.0 + zv * (1.0 - q)))
        DYE[r, :] = (dy.astype(F32) * ENT[r, :]).astype(BF16)
        shifted = pl.ds(pl.multiple_of(8 + i * CH, 8), CH)
        XF[shifted, :] = xraw[r, :].astype(F32)
        BCF[shifted, :] = bcr[r, :].astype(F32)
        return carry

    lax.fori_loop(0, T // CH, gates, 0)

    pl.semaphore_wait(barrier, nseq - 1 + nz - 1 + 2)

    halo_x = send(xraw.at[T - 16 :], HXR, s_h.at[0], r_h.at[0], at_seq(s + 1))
    halo_b = send(bcr.at[T - 16 :], HBR, s_h.at[1], r_h.at[1], at_seq(s + 1))

    @pl.when(s < nseq - 1)
    def _():
        halo_x.start()
        halo_b.start()

    def conv_chunk(i, carry):
        r = blk(i, CH)
        ext = pl.ds(pl.multiple_of(i * CH, 8), CH + 8)

        def pre(F, taps):
            v = F[ext, :]
            out = taps[0:1, :] * v[8:, :]
            for k in range(1, TAPS):
                out = out + taps[k : k + 1, :] * pltpu.roll(v, k, 0)[8:, :]
            return out

        v = pre(BCF, cvb)
        q = sigmoid(v)
        BCP[r, :] = (v * q).astype(BF16)
        BCS[r, :] = q * (1.0 + v * (1.0 - q))
        v = pre(XF, cvx)
        q = sigmoid(v)
        post = (v * q).astype(BF16)
        XP[r, :] = post
        XS[r, :] = q * (1.0 + v * (1.0 - q))
        wx = (post.astype(F32) * DTE[r, :]).astype(BF16)
        WX[r, :] = wx
        WL[r, :] = (wx.astype(F32) * LEA[r, :]).astype(BF16)
        return carry

    per = BLOCK // CH
    N = W // 2

    def block_ends(k, carry):
        EK[k] = mm(BCP[blk(k), :N], WL[blk(k), :], TN)
        BK[k] = mm(BCP[blk(k), N:], DYE[blk(k), :], TN)
        return carry

    lax.fori_loop(per, nb * per, conv_chunk, 0)
    lax.fori_loop(1, nb, block_ends, 0)

    @pl.when(s > 0)
    def _():
        halo_x.wait_recv()
        halo_b.wait_recv()
        XF[0:8, :] = HXR[8:16, :].astype(F32)
        BCF[0:8, :] = HBR[8:16, :].astype(F32)

    @pl.when(s == 0)
    def _():
        XF[0:8, :] = jnp.zeros((8, W), F32)
        BCF[0:8, :] = jnp.zeros((8, W), F32)

    lax.fori_loop(0, per, conv_chunk, 0)
    block_ends(0, 0)

    state = jnp.zeros((N, W), F32)
    for k in range(nb):
        LS[k] = state
        state = jnp.exp(-TOT[k][0:1, :]) * state + EK[k]
    grad = jnp.zeros((N, W), F32)
    for k in reversed(range(nb)):
        NS[k] = grad
        grad = jnp.exp(-TOT[k][0:1, :]) * grad + BK[k]
    dtot = TOT[0]
    for k in range(1, nb):
        dtot = dtot + TOT[k]
    q1, q2, q3 = (p.astype(F32) for p in parts3(dtot[0:1, :]))
    rt = lax.broadcasted_iota(jnp.int32, (16, W), 0)
    tail = jnp.where(rt == 0, q1, jnp.where(rt == 1, q2, jnp.where(rt == 2, q3, 0.0)))
    tail = tail.astype(BF16)
    EB[0, 0:N, :] = state.astype(BF16)
    EB[1, 0:N, :] = grad.astype(BF16)
    EB[0, N : N + 16, :] = tail
    EB[1, N : N + 16, :] = tail

    def state_copy(d):
        p, wrapped = other(d)
        return send(EB.at[wrapped], SLOT.at[s], s_st.at[d], r_st.at[s], at_seq(p))

    for d in range(1, nseq):
        state_copy(d).start()

    lane_h = lax.broadcasted_iota(jnp.int32, (BLOCK, W), 1) // HEAD_DIM
    r512 = lax.rem(lax.broadcasted_iota(jnp.int32, (3 * n16, heads * 128), 0), n16)
    l512 = lax.broadcasted_iota(jnp.int32, (3 * n16, heads * 128), 1) // 128
    for h in range(heads):
        KH[0:128, h * BLOCK + 128 : (h + 1) * BLOCK] = jnp.zeros((128, 128), BF16)
    TQ = 64

    def inside(k, carry):
        bm, cm = BCP[blk(k), :N], BCP[blk(k), N:]
        wx, dy = WX[blk(k), :], DY[blk(k), :]
        for h in range(heads):
            WXM[h * BLOCK : (h + 1) * BLOCK, :] = jnp.where(lane_h == h, wx, jnp.zeros_like(wx))
            DYM[h * BLOCK : (h + 1) * BLOCK, :] = jnp.where(lane_h == h, dy, jnp.zeros_like(dy))
        hot = ((r512 // heads == k) & (lax.rem(r512, heads) == l512)).astype(F32).astype(BF16)
        col = mm(WP[...], hot, TN)
        for t0 in range(0, BLOCK, TQ):
            ext = 128 if t0 < 128 else BLOCK
            sc = mm(cm[t0 : t0 + TQ, :], bm[0:ext, :], NT)
            tt = t0 + lax.broadcasted_iota(jnp.int32, (TQ, ext), 0)
            ss = lax.broadcasted_iota(jnp.int32, (TQ, ext), 1)
            keep = tt >= ss
            total = None
            for h in range(heads):
                wrow = GC[pl.ds(k * heads + h, 1), :][:, 0:ext]
                wcol = col[t0 : t0 + TQ, h * 128 : (h + 1) * 128]
                if ext > 128:
                    wcol = jnp.concatenate([wcol, wcol], axis=1)
                decay = jnp.where(keep, jnp.exp(jnp.minimum(wrow - wcol, 0.0)), 0.0)
                KH[t0 : t0 + TQ, h * BLOCK : h * BLOCK + ext] = (sc * decay).astype(BF16)
                mixing = mm(DYM[h * BLOCK + t0 : h * BLOCK + t0 + TQ, :], wx[0:ext, :], NT)
                part = mixing * decay
                total = part if total is None else total + part
            rows = pl.ds(pl.multiple_of(k * BLOCK + t0, TQ), TQ)
            MX[rows, 0:ext] = total.astype(BF16)
            if ext < BLOCK:
                MX[rows, ext:] = jnp.zeros((TQ, BLOCK - ext), BF16)
        YIN[blk(k), :] = mm(KH[...], WXM[...])
        acc = None
        for h in range(heads):
            part = mm(KH[:, h * BLOCK : (h + 1) * BLOCK], DYM[h * BLOCK : (h + 1) * BLOCK, :], TN)
            acc = part if acc is None else acc + part
        WGIN[blk(k), :] = acc
        return carry

    lax.fori_loop(0, nb, inside, 0)

    for d in range(1, nseq):
        p, _ = other(d)
        send(EB.at[0], SLOT.at[p], s_st.at[d], r_st.at[p], at_seq(p)).wait_recv()

    def fold(p, value):
        t3 = SLOT[p, N : N + 16, :].astype(F32)
        dec = jnp.exp(-(t3[0:1, :] + t3[1:2, :] + t3[2:3, :]))
        return dec * value + SLOT[p, 0:N, :].astype(F32)

    s_in = lax.fori_loop(0, s, fold, jnp.zeros((N, W), F32))
    g_in = lax.fori_loop(0, nseq - 1 - s, lambda i, v: fold(nseq - 1 - i, v), jnp.zeros((N, W), F32))
    before = jnp.zeros((1, W), F32)
    for k in range(nb):
        SB[k] = (LS[k] + jnp.exp(-before) * s_in).astype(BF16)
        before = before + TOT[k][0:1, :]
    after = jnp.zeros((1, W), F32)
    for k in reversed(range(nb)):
        GB[k] = (NS[k] + jnp.exp(-after) * g_in).astype(BF16)
        after = after + TOT[k][0:1, :]

    def shared(k, carry):
        r = blk(k)
        mx = MX[r, :]
        bg = mm(mx, BCP[r, N:], TN) + mm(WL[r, :], GB[k], NT)
        cg = mm(mx, BCP[r, :N]) + mm(DYE[r, :], SB[k], NT)
        BS[r, :N] = bg * BCS[r, :N]
        BS[r, N:] = cg * BCS[r, N:]
        return carry

    shared(0, 0)
    HSB[0] = BS[0:8, :]
    halo_bs = send(HSB.at[0], HSB.at[1], s_sl.at[0], r_sl.at[0], at_seq(s - 1))

    @pl.when(s > 0)
    def _():
        halo_bs.start()

    lax.fori_loop(1, nb, shared, 0)

    def tap_sums(slope, F, start, carry):
        n = slope.shape[0]
        v = F[pl.ds(pl.multiple_of(start, 8), n + 8), :]
        out = []
        for k in range(TAPS):
            moved = v[8:, :] if k == 0 else pltpu.roll(v, k, 0)[8:, :]
            out.append(carry[k] + (slope * moved).reshape(n // 8, 8, W).sum(axis=0))
        return tuple(out)

    def stack_taps(sums):
        rt8 = lax.broadcasted_iota(jnp.int32, (8, W), 0)
        out = jnp.zeros((8, W), F32)
        for k in range(TAPS):
            out = jnp.where(rt8 == k, jnp.sum(sums[k], axis=0, keepdims=True), out)
        return out

    zero4 = tuple(jnp.zeros((8, W), F32) for _ in range(TAPS))
    sums = lax.fori_loop(
        0, T // CH, lambda i, cr: tap_sums(BS[blk(i, CH), :], BCF, i * CH, cr), zero4
    )
    CBS[s] = stack_taps(sums)

    def seq_copy(buf, d, ss, rs):
        p, _ = other(d)
        return send(buf.at[s], buf.at[s], ss.at[d], rs.at[s], at_seq(p))

    def seq_wait(buf, ss, rs):
        for d in range(1, nseq):
            p, _ = other(d)
            send(buf.at[p], buf.at[p], ss.at[d], rs.at[p], at_seq(p)).wait_recv()

    for d in range(1, nseq):
        seq_copy(CBS, d, s_cb, r_cb).start()

    groups = nz * nyl * nc
    per_block = groups // nb
    zy_block = per_block // nc

    def bc_adjoint(j, carry):
        u = BS[pl.ds(pl.multiple_of(j * own, 8), own + 8), :]
        out = cvb[0:1, :] * u[:own, :]
        for k in range(1, TAPS):
            out = out + cvb[k : k + 1, :] * pltpu.roll(u, own + 8 - k, 0)[:own, :]
        PR[j // nc, lax.rem(j, nc)] = out.astype(BF16)
        return carry

    def a_copy(q):
        part = pl.ds(q * zy_block, zy_block)
        return send(PR.at[part, 1 - c], RA.at[part], s_a.at[q], r_a.at[q], core_dev)

    for q in range(nb):
        if q == nb - 1:

            @pl.when(s < nseq - 1)
            def _():
                halo_bs.wait_recv()
                BS[T : T + 8, :] = HSB[1]

            @pl.when(s == nseq - 1)
            def _():
                BS[T : T + 8, :] = jnp.zeros((8, W), F32)

        lax.fori_loop(q * per_block, (q + 1) * per_block, bc_adjoint, 0)
        a_copy(q).start()

    CW = 128
    lane1 = lax.broadcasted_iota(jnp.int32, (1, W), 1) // HEAD_DIM
    skip = by_head([d_s[h] for h in range(heads)], lane1)
    pick = (
        lax.broadcasted_iota(jnp.int32, (16, W), 0)
        == lax.broadcasted_iota(jnp.int32, (16, W), 1) // HEAD_DIM
    ).astype(F32).astype(BF16)

    def channels(i, carry):
        r = blk(i, CW)
        k = i // (BLOCK // CW)
        wg = WGIN[r, :] + LEA[r, :] * mm(BCP[r, :N], GB[k])
        xp = XP[r, :].astype(F32)
        slope = (DTE[r, :] * wg + skip * DY[r, :].astype(F32)) * XS[r, :]
        XSL[r, :] = slope
        prod = xp * wg
        hi = prod.astype(BF16)
        lo = (prod - hi.astype(F32)).astype(BF16)
        steps = mm(pick, hi, NT) + mm(pick, lo, NT)
        sg_o[:, pl.ds(pl.multiple_of(i * CW, CW), CW)] = steps[0:heads, :]
        return tap_sums(slope, XF, i * CW, carry)

    sums = channels(0, zero4)
    HSX[0] = XSL[0:8, :]
    halo_xs = send(HSX.at[0], HSX.at[1], s_sl.at[1], r_sl.at[1], at_seq(s - 1))

    @pl.when(s > 0)
    def _():
        halo_xs.start()

    def b_step(q):
        zs = nz // nb
        for zi in range(zs):
            zz = q * zs + zi
            A1S[zz] = (
                PR[zz * nyl + 1 - yl, c].astype(F32) + RA[zz * nyl + 1 - yl].astype(F32)
            ).astype(BF16)
            A1K[zz] = PR[zz * nyl + yl, c].astype(F32) + RA[zz * nyl + yl].astype(F32)

    def b_copy(q):
        part = pl.ds(q * (nz // nb), nz // nb)
        return send(A1S.at[part], RB.at[part], s_b.at[q], r_b.at[q], y_dev)

    per_q = (T // CW) // nb
    for q in range(nb):
        sums = lax.fori_loop(max(1, q * per_q), (q + 1) * per_q, channels, sums)
        a_copy(q).wait_recv()
        b_step(q)
        b_copy(q).start()
    CXS[s] = stack_taps(sums)
    for d in range(1, nseq):
        seq_copy(CXS, d, s_cx, r_cx).start()

    def total8(buf, n):
        out = buf[0]
        for p in range(1, n):
            out = out + buf[p]
        return out

    seq_wait(CBS, s_cb, r_cb)
    CBL[0] = total8(CBS, nseq)
    cc_copy = send(CBL.at[0], CBL.at[1], s_cc.at[0], r_cc.at[0], core_dev)
    cc_copy.start()

    def outputs(i, carry):
        r = blk(i, CH)
        k = i // (BLOCK // CH)
        y = YIN[r, :] + ENT[r, :] * mm(BCP[r, N:], SB[k]) + skip * XP[r, :].astype(F32)
        gg_o[r, :] = (GZ[r, :] * y).astype(BF16)
        return carry

    lax.fori_loop(0, T // CH // 2, outputs, 0)

    for q in range(nb):
        b_copy(q).wait_recv()
    for zz in range(nz):
        val = A1K[zz] + RB[zz].astype(F32)
        A2[zz] = val
        ZS[zz] = val.astype(BF16)

    def z_copy(d):
        t = other_z(d)
        return send(ZS.at[t], RZ.at[z], s_z.at[d], r_z.at[z], {"head_0": t})

    for d in range(1, nz):
        z_copy(d).start()

    cc_copy.wait_recv()
    CBT[0] = CBL[0] + CBL[1]
    cy_copy = send(CBT.at[0], CBT.at[1], s_cc.at[1], r_cc.at[1], y_dev)
    cy_copy.start()

    lax.fori_loop(T // CH // 2, T // CH, outputs, 0)

    def x_adjoint(i, carry):
        r = blk(i, CH)
        u = XSL[pl.ds(pl.multiple_of(i * CH, 8), CH + 8), :]
        out = cvx[0:1, :] * u[:CH, :]
        for k in range(1, TAPS):
            out = out + cvx[k : k + 1, :] * pltpu.roll(u, CH + 8 - k, 0)[:CH, :]
        xg_o[r, :] = out.astype(BF16)
        return carry

    @pl.when(s < nseq - 1)
    def _():
        halo_xs.wait_recv()
        XSL[T : T + 8, :] = HSX[1]

    @pl.when(s == nseq - 1)
    def _():
        XSL[T : T + 8, :] = jnp.zeros((8, W), F32)

    cy_copy.wait_recv()
    CBZ[z] = CBT[0] + CBT[1]

    def cz_copy(d):
        return send(CBZ.at[z], CBZ.at[z], s_cz.at[d], r_cz.at[z], {"head_0": other_z(d)})

    for d in range(1, nz):
        cz_copy(d).start()

    lax.fori_loop(0, T // CH, x_adjoint, 0)

    seq_wait(CXS, s_cx, r_cx)
    cx_o[...] = total8(CXS, nseq)[0:TAPS, :]
    out = A2[z]
    for d in range(1, nz):
        t = other_z(d)
        send(ZS.at[t], RZ.at[t], s_z.at[d], r_z.at[t], {"head_0": t}).wait_recv()
        out = out + RZ[t].astype(F32)
    bg_o[...] = out
    for d in range(1, nz):
        t = other_z(d)
        send(CBZ.at[t], CBZ.at[t], s_cz.at[d], r_cz.at[t], {"head_0": t}).wait_recv()
    cb_o[...] = total8(CBZ, nz)[0:TAPS, :]

    @pl.when(s < nseq - 1)
    def _():
        halo_x.wait_send()
        halo_b.wait_send()

    @pl.when(s > 0)
    def _():
        halo_bs.wait_send()
        halo_xs.wait_send()

    for d in range(1, nseq):
        state_copy(d).wait_send()
        seq_copy(CBS, d, s_cb, r_cb).wait_send()
        seq_copy(CXS, d, s_cx, r_cx).wait_send()
    for q in range(nb):
        a_copy(q).wait_send()
        b_copy(q).wait_send()
    for d in range(1, nz):
        z_copy(d).wait_send()
        cz_copy(d).wait_send()
    cc_copy.wait_send()
    cy_copy.wait_send()


def local(dims, xraw, zgate, bcraw, dt, a_rate, d_skip, conv_x, conv_bc, dout):
    nx, nyh, nz, nyl, nc = dims
    nseq = nx * nyh
    T, W = xraw.shape
    nb = T // BLOCK
    heads = W // HEAD_DIM
    N = W // 2
    own = T // (nz * nyl * nc)
    vm = lambda *shape: pltpu.VMEM(shape[:-1], shape[-1])
    full, half = vm(T, W, F32), vm(T, W, BF16)
    ext = vm(T + 8, W, F32)
    dma = lambda n: pltpu.SemaphoreType.DMA((n,))
    scratch = (
        [ext, ext] + [full] * 8 + [ext, ext]
        + [half] * 5 + [half, vm(T, BLOCK, BF16)]
        + [vm(nb * heads, BLOCK, F32), vm(nb * heads, BLOCK, F32), vm(3 * nb * heads, BLOCK, BF16)]
        + [vm(nb, 8, W, F32)]
        + [vm(nb, N, W, F32)] * 4
        + [vm(nb, N, W, BF16)] * 2
        + [vm(2, N + 16, W, BF16), vm(nseq, N + 16, W, BF16)]
        + [vm(BLOCK, heads * BLOCK, BF16), vm(heads * BLOCK, W, BF16), vm(heads * BLOCK, W, BF16)]
        + [vm(16, W, BF16)] * 2 + [vm(2, 8, W, F32)] * 2
        + [vm(nz * nyl, nc, own, W, BF16), vm(nz * nyl, own, W, BF16)]
        + [vm(nz, own, W, BF16), vm(nz, own, W, F32), vm(nz, own, W, BF16), vm(nz, own, W, F32)]
        + [vm(nz, own, W, BF16), vm(nz, own, W, BF16)]
        + [vm(nseq, 8, W, F32)] * 2 + [vm(2, 8, W, F32)] * 2 + [vm(nz, 8, W, F32)]
        + [dma(2)] * 2 + [dma(nseq)] * 2 + [dma(2)] * 2 + [dma(nb)] * 4 + [dma(nz)] * 2
        + [dma(nseq)] * 4 + [dma(2)] * 2 + [dma(nz)] * 2
    )
    vspec = pl.BlockSpec(memory_space=pltpu.VMEM)
    sspec = pl.BlockSpec(memory_space=pltpu.SMEM)
    return pl.pallas_call(
        functools.partial(kernel, dims, T, W),
        name="ssd_backward",
        out_shape=(
            jax.ShapeDtypeStruct((T, W), BF16),
            jax.ShapeDtypeStruct((T, W), BF16),
            jax.ShapeDtypeStruct((heads, T), F32),
            jax.ShapeDtypeStruct((own, W), F32),
            jax.ShapeDtypeStruct((TAPS, W), F32),
            jax.ShapeDtypeStruct((TAPS, W), F32),
        ),
        in_specs=[vspec, vspec, vspec, vspec, sspec, sspec, vspec, vspec, vspec],
        out_specs=tuple([vspec] * 6),
        scratch_shapes=scratch,
        compiler_params=pltpu.CompilerParams(
            collective_id=0, has_side_effects=True, vmem_limit_bytes=56 * 1024 * 1024
        ),
    )(xraw, zgate, bcraw, dt, a_rate, d_skip, conv_x, conv_bc, dout)


def over_mesh(torus):
    placed = (
        P(SEQ, HEAD), P(SEQ, HEAD), P(SEQ, None), P(HEAD, SEQ), P(HEAD), P(HEAD),
        P(None, HEAD), P(), P(SEQ, HEAD),
    )
    return jax.shard_map(
        functools.partial(local, tuple(torus.devices.shape)),
        mesh=torus,
        in_specs=placed,
        out_specs=(P(SEQ, HEAD), P(SEQ, HEAD), P(HEAD, SEQ), P(SEQ_HEAD, None), P(None, HEAD), P()),
        check_vma=False,
    )


def solution(mesh):
    return over_mesh(Mesh(mesh.devices.reshape(4, 2, 8, 2, 2), SEQ_HEAD))
```

time: 176 us -> 49.9 us (0.28)
  starting transfers between devices: 55 us -> 0 us
  Pallas kernels: 0 us -> 43 us
  blocking collectives: 31.9 us -> 0 us
  other arithmetic: 26.2 us -> 0 us
  local copies, waits for them, and re-layouts: 30.3 us -> 5.43 us
  matrix products: 21.9 us -> 0 us
  waiting for transfers between devices: 8.42 us -> 0 us
    pallas_call x0 -> x1, Pallas kernels: none -> 43 us  [local(): pl.pallas_call(functools.partial(kernel, dims, T, W), name='ssd_backward'...]
    all_to_all x5 -> x0, starting transfers between devices: 38 us -> none  [the longest x4 24.1 us: sent_to_all(): lax.all_to_all(jnp.broadcast_to(x[None], (length, *x.shape)), axis, 0, 0,...]
    psum x5 -> x0, blocking collectives: 31.9 us -> none  [by_axis(): x = lax.psum(x, axis)]
    dot_general x14 -> x0, matrix products: 21.3 us -> none  [the longest x1 3.73 us: local(): jnp.einsum('hcts,cshp->cthp', kernel, w_blocks, preferred_element_type=jn...]
    ppermute x3 -> x0, starting transfers between devices: 17.1 us -> none  [from_behind(): lax.ppermute(value, axis, [(source, source + steps) for source in range(i...]
    slice x27 -> x0, local copies, waits for them, and re-layouts: 8.9 us -> none  [the longest x17 4.98 us: combined_pairwise(): part[side::2]]
    convert_element_type x6 -> x0, local copies, waits for them, and re-layouts: 8.48 us -> none  [the longest x2 3.92 us: local(): dout.reshape(block_count, block_len, head_count, head_size)]
    all_to_all x5 -> x0, waiting for transfers between devices: 8.41 us -> none  [the longest x1 5.56 us: sum_at_owner(): tiles = lax.all_to_all(in_blocks(x, dim, length), axis, 0, 0, tiled=True)]
  transfers between devices with their start and end apart: 8 -> 0, of which waited for: 3 -> 0; matrix products, arithmetic and copies ran while one was open for 33% -> 0% of each run, Pallas kernels for 0% -> 0%
where the time goes in v1:
time: 49.9 us; the launch traced here: 49.1 us
  Pallas kernels  43 us (86%)
  local copies, waits for them, and re-layouts  5.43 us (11%)
  between operations  0.66 us (1%)
    pallas_call x1, Pallas kernels, local(): pl.pallas_call(functools.partial(kernel, dims, T, W), name='ssd_backward'...  43 us
    unnamed x16, local copies, waits for them, and re-layouts  5.43 us

profile of v1, /device:TPU:1, one launch (start us, length us, event | category | flops | bytes accessed | tf_op | source)
XLA Modules:
  0.0 49.1 jit_solution(5215358264908063566)
XLA Ops:
  0.6 43.0 %ssd_backward.1 = (bf16[1024,256]{1,0:T(8,128)(2,1)}, bf16[1024,256]{1,0:T(8,128)(2,1)}, f32[4,1024]{1,0:T(4,128)}, f32[32,256]{1,0:T(8,128)}, f32[4,256]{1,0:T(4,128)}, /*index=5*/f32[4,256]{1,0:T(4,128)}) custom-call(bf16[1024,256]{1,0:T(8,128)(2,1)} %xraw.1, bf16[1024,256]{1,0:T(8,128)(2,1)} %zg.1, bf16[1024,256]{1,0:T(8,128)(2,1)} %bcr.1, f32[4,1024]{1,0:T(4,128)} %dt.1, ...), custom_call_target="tpu_custom_call" | custom-call | tf_op jit(solution)/shard_map/ssd_backward/pallas_call | solution.py:580
  43.7 0.0 copy-start
  43.7 1.9 %copy.21 = bf16[1024,256]{1,0:T(8,128)(2,1)} copy(bf16[1024,256]{1,0:T(8,128)(2,1)} %get-tuple-element.12) | data formatting | bytes 1048576
  45.6 0.0 copy-done
  45.6 0.0 copy-start.2
  45.6 0.8 %copy.22 = bf16[1024,256]{1,0:T(8,128)(2,1)} copy(bf16[1024,256]{1,0:T(8,128)(2,1)S(1)} %copy-done) | data formatting | bytes 1048576
  46.4 0.0 copy-done.2
  46.4 0.0 copy-start.1
  46.4 0.6 %copy.23 = f32[4,1024]{1,0:T(4,128)} copy(f32[4,1024]{1,0:T(4,128)S(1)} %copy-done.2) | data formatting | bytes 32768
  47.0 0.2 copy-done.1
  47.2 0.0 copy-start.4
  47.2 0.6 %copy.24 = f32[32,256]{1,0:T(8,128)} copy(f32[32,256]{1,0:T(8,128)S(1)} %copy-done.1) | data formatting | bytes 65536
  47.8 0.1 copy-done.4
  47.9 0.0 copy-start.3
  47.9 0.6 %copy.25 = f32[4,256]{1,0:T(4,128)} copy(f32[4,256]{1,0:T(4,128)S(1)} %copy-done.4) | data formatting | bytes 8192
  48.5 0.1 copy-done.3
  48.5 0.6 %copy.26 = f32[4,256]{1,0:T(4,128)} copy(f32[4,256]{1,0:T(4,128)S(1)} %copy-done.3) | data formatting | bytes 8192
Async XLA Ops:
  43.7 1.9 %copy-start = (bf16[1024,256]{1,0:T(8,128)(2,1)S(1)}, bf16[1024,256]{1,0:T(8,128)(2,1)}, u32[]{:S(2)}) copy-start(bf16[1024,256]{1,0:T(8,128)(2,1)} %get-tuple-element.13) | copy-start | bytes 1572868
  45.6 0.8 %copy-start.2 = (f32[4,1024]{1,0:T(4,128)S(1)}, f32[4,1024]{1,0:T(4,128)}, u32[]{:S(2)}) copy-start(f32[4,1024]{1,0:T(4,128)} %get-tuple-element.14) | copy-start | bytes 49156
  46.4 0.8 %copy-start.1 = (f32[32,256]{1,0:T(8,128)S(1)}, f32[32,256]{1,0:T(8,128)}, u32[]{:S(2)}) copy-start(f32[32,256]{1,0:T(8,128)} %get-tuple-element.15) | copy-start | bytes 98308
  47.2 0.7 %copy-start.4 = (f32[4,256]{1,0:T(4,128)S(1)}, f32[4,256]{1,0:T(4,128)}, u32[]{:S(2)}) copy-start(f32[4,256]{1,0:T(4,128)} %get-tuple-element.16) | copy-start | bytes 12292
  47.9 0.7 %copy-start.3 = (f32[4,256]{1,0:T(4,128)S(1)}, f32[4,256]{1,0:T(4,128)}, u32[]{:S(2)}) copy-start(f32[4,256]{1,0:T(4,128)} %get-tuple-element.17) | copy-start | bytes 12292

commit v2 on v1

v2 whole, which is shorter than its diff:
```python
import functools

import jax
import jax.numpy as jnp
from jax import lax
from jax.experimental import pallas as pl
from jax.experimental.pallas import tpu as pltpu
from jax.sharding import Mesh
from jax.sharding import PartitionSpec as P

HEAD_DIM = 64
BLOCK = 256
TAPS = 4
SEQ = ("seq_0", "seq_1")
HEAD = ("head_0", "head_1", "head_2")
SEQ_HEAD = SEQ + HEAD
F32, BF16 = jnp.float32, jnp.bfloat16


def mm(a, b, dims=((1,), (0,))):
    return lax.dot_general(a, b, (dims, ((), ())), preferred_element_type=F32)


NT = ((1,), (1,))
TN = ((0,), (0,))


def parts3(v):
    p1 = v.astype(BF16)
    r1 = v - p1.astype(F32)
    p2 = r1.astype(BF16)
    r2 = r1 - p2.astype(F32)
    return p1, p2, r2.astype(BF16)


def sigmoid(v):
    return 0.5 * jnp.tanh(0.5 * v) + 0.5


def silu_slope(v):
    q = sigmoid(v)
    return q * (1.0 + v * (1.0 - q))


def by_head(scalars, lanes):
    out = jnp.full(lanes.shape, scalars[3], F32)
    for h in (2, 1, 0):
        out = jnp.where(lanes == h, scalars[h], out)
    return out


def kernel(
    dims, T, W,
    xraw_h, zg_h, bcr_h, dt_h, a_s, d_s, cvx_h, cvb_h, dout_h,
    xg_o, gg_o, sg_o, bg_o, cx_o, cb_o,
    xraw, zg, bcr, dt, cvx, cvb, dout,
    XF, BCF, XS, BCS, GZ, DTE, ENT, LEA, YIN, WGIN, XSL, BS,
    XP, WX, WL, DY, DYE, BCP, MX,
    GC, DC, WP, TOT, EK, BK, LS, NS, SB, GB, EB, SLOT, CR, CSLOT,
    KH, WXM, DYM, HXR, HBR, HSX, HSB,
    PR, RA, ZS, RZ, CXS, CBS, CBL, CBZ,
    s_in, s_h, r_h, s_st, r_st, s_cr, r_cr, s_sl, r_sl, s_a, r_a, s_z, r_z,
    s_cx, r_cx, s_cb, r_cb, s_cc, r_cc, s_cz, r_cz,
):
    nx, nyh, nz, nyl, nc = dims
    nseq = nx * nyh
    nzy = nz * nyl
    nb = T // BLOCK
    heads = W // HEAD_DIM
    own = T // (nzy * nc)
    sx, sy = lax.axis_index("seq_0"), lax.axis_index("seq_1")
    s = sx * nyh + sy
    z, yl, c = (lax.axis_index(n) for n in HEAD)
    m = z * nyl + yl

    def at_seq(p):
        return {"seq_0": p // nyh, "seq_1": lax.rem(p, nyh)}

    def at_zy(p):
        return {"head_0": p // nyl, "head_1": lax.rem(p, nyl)}

    def other(d):
        wrapped = (s + d) // nseq
        return s + d - nseq * wrapped, wrapped

    def other_zy(d):
        return lax.rem(m + d, nzy)

    far_first = sorted(range(1, nzy), key=lambda d: -min(d, nzy - d))

    def send(src, dst, ss, rs, dev):
        return pltpu.make_async_remote_copy(
            src_ref=src, dst_ref=dst, send_sem=ss, recv_sem=rs,
            device_id=dev, device_id_type=pl.DeviceIdType.MESH,
        )

    core_dev = {"head_2": 1 - c}

    barrier = pltpu.get_barrier_semaphore()

    def greet(dev):
        pl.semaphore_signal(barrier, inc=1, device_id=dev, device_id_type=pl.DeviceIdType.MESH)

    for d in range(1, nseq):
        greet(at_seq(other(d)[0]))
    for d in far_first:
        greet(at_zy(other_zy(d)))
    greet(core_dev)

    loads = [
        pltpu.make_async_copy(a, b, s_in.at[i])
        for i, (a, b) in enumerate(
            [(dt_h, dt), (zg_h, zg), (dout_h, dout), (bcr_h, bcr), (xraw_h, xraw),
             (cvx_h, cvx), (cvb_h, cvb)]
        )
    ]
    for load in loads:
        load.start()

    rows16 = lax.broadcasted_iota(jnp.int32, (heads, BLOCK), 0)
    a_col = by_head([a_s[h] for h in range(heads)], rows16)
    n16 = nb * heads
    ri = lax.broadcasted_iota(jnp.int32, (BLOCK, BLOCK), 0)
    ci = lax.broadcasted_iota(jnp.int32, (BLOCK, BLOCK), 1)
    tri = (ri <= ci).astype(F32).astype(BF16)
    rr = lax.rem(lax.broadcasted_iota(jnp.int32, (3 * n16, W), 0), n16)
    ll = lax.broadcasted_iota(jnp.int32, (3 * n16, W), 1) // HEAD_DIM
    loads[0].wait()
    for k in range(nb):
        piece = dt[:, k * BLOCK : (k + 1) * BLOCK]
        DC[k * heads : (k + 1) * heads, :] = piece
        GC[k * heads : (k + 1) * heads, :] = piece * a_col
    w3 = mm(jnp.concatenate(parts3(GC[...]), axis=0), tri)
    within = w3[:n16] + w3[n16 : 2 * n16] + w3[2 * n16 :]
    GC[...] = within
    wp = jnp.concatenate(parts3(within), axis=0)
    dp = jnp.concatenate(parts3(DC[...]), axis=0)
    WP[...] = wp

    def blk(k, n=BLOCK):
        return pl.ds(pl.multiple_of(k * n, n), n)

    def expand(k, carry):
        hot = ((rr // heads == k) & (lax.rem(rr, heads) == ll)).astype(F32).astype(BF16)
        wexp = mm(wp, hot, TN)
        total = wexp[BLOCK - 1 : BLOCK, :]
        TOT[k] = jnp.broadcast_to(total, (8, W))
        ENT[blk(k), :] = jnp.exp(-wexp)
        LEA[blk(k), :] = jnp.exp(jnp.minimum(wexp - total, 0.0))
        DTE[blk(k), :] = mm(dp, hot, TN)
        return carry

    lax.fori_loop(0, nb, expand, 0)

    CH = 64
    N = W // 2
    per = BLOCK // CH
    for load in loads[1:]:
        load.wait()
    XF[0:8, :] = jnp.zeros((8, W), F32)
    BCF[0:8, :] = jnp.zeros((8, W), F32)

    def gates(i, carry):
        r = blk(i, CH)
        zv = zg[r, :].astype(F32)
        dy = (dout[r, :].astype(F32) * (zv * sigmoid(zv))).astype(BF16)
        DY[r, :] = dy
        DYE[r, :] = (dy.astype(F32) * ENT[r, :]).astype(BF16)
        shifted = pl.ds(pl.multiple_of(8 + i * CH, 8), CH)
        XF[shifted, :] = xraw[r, :].astype(F32)
        BCF[shifted, :] = bcr[r, :].astype(F32)
        return carry

    lax.fori_loop(0, T // CH, gates, 0)

    def conv_chunk(i, carry):
        r = blk(i, CH)
        ext = pl.ds(pl.multiple_of(i * CH, 8), CH + 8)

        def pre(F, taps):
            v = F[ext, :]
            out = taps[0:1, :] * v[8:, :]
            for k in range(1, TAPS):
                out = out + taps[k : k + 1, :] * pltpu.roll(v, k, 0)[8:, :]
            return out

        v = pre(BCF, cvb)
        BCP[r, :] = (v * sigmoid(v)).astype(BF16)
        BCS[r, :] = v
        v = pre(XF, cvx)
        post = (v * sigmoid(v)).astype(BF16)
        XP[r, :] = post
        XS[r, :] = v
        wx = (post.astype(F32) * DTE[r, :]).astype(BF16)
        WX[r, :] = wx
        WL[r, :] = (wx.astype(F32) * LEA[r, :]).astype(BF16)
        return carry

    def block_ends(k, carry):
        EK[k] = mm(BCP[blk(k), :N], WL[blk(k), :], TN)
        BK[k] = mm(BCP[blk(k), N:], DYE[blk(k), :], TN)
        return carry

    lax.fori_loop(0, T // CH, conv_chunk, 0)
    rt = lax.broadcasted_iota(jnp.int32, (16, W), 0)
    edge = rt < TAPS - 1
    BCP[0:16, :] = jnp.where(edge, jnp.zeros((16, W), BF16), BCP[0:16, :])
    lax.fori_loop(0, nb, block_ends, 0)

    state = jnp.zeros((N, W), F32)
    for k in range(nb):
        LS[k] = state
        state = jnp.exp(-TOT[k][0:1, :]) * state + EK[k]
    EB[0] = state.astype(BF16)
    grad = jnp.zeros((N, W), F32)
    for k in reversed(range(nb)):
        NS[k] = grad
        grad = jnp.exp(-TOT[k][0:1, :]) * grad + BK[k]
    EB[1] = grad.astype(BF16)

    pl.semaphore_wait(barrier, nseq - 1 + nzy - 1 + 1)

    halo_x = send(xraw.at[T - 16 :], HXR, s_h.at[0], r_h.at[0], at_seq(s + 1))
    halo_b = send(bcr.at[T - 16 :], HBR, s_h.at[1], r_h.at[1], at_seq(s + 1))

    @pl.when(s < nseq - 1)
    def _():
        halo_x.start()
        halo_b.start()

    def state_copy(d):
        p, wrapped = other(d)
        return send(EB.at[wrapped], SLOT.at[s], s_st.at[d], r_st.at[s], at_seq(p))

    def edge_copy(d):
        p, wrapped = other(d)
        return send(CR.at[wrapped], CSLOT.at[s], s_cr.at[d], r_cr.at[s], at_seq(p))

    for d in range(1, nseq):
        state_copy(d).start()

    lane_h = lax.broadcasted_iota(jnp.int32, (BLOCK, W), 1) // HEAD_DIM
    r512 = lax.rem(lax.broadcasted_iota(jnp.int32, (3 * n16, heads * 128), 0), n16)
    l512 = lax.broadcasted_iota(jnp.int32, (3 * n16, heads * 128), 1) // 128
    for h in range(heads):
        KH[0:128, h * BLOCK + 128 : (h + 1) * BLOCK] = jnp.zeros((128, 128), BF16)
    TQ = 64

    def inside(k, carry):
        bm, cm = BCP[blk(k), :N], BCP[blk(k), N:]
        wx, dy = WX[blk(k), :], DY[blk(k), :]
        for h in range(heads):
            WXM[h * BLOCK : (h + 1) * BLOCK, :] = jnp.where(lane_h == h, wx, jnp.zeros_like(wx))
            DYM[h * BLOCK : (h + 1) * BLOCK, :] = jnp.where(lane_h == h, dy, jnp.zeros_like(dy))
        hot = ((r512 // heads == k) & (lax.rem(r512, heads) == l512)).astype(F32).astype(BF16)
        col = mm(WP[...], hot, TN)
        for t0 in range(0, BLOCK, TQ):
            ext = 128 if t0 < 128 else BLOCK
            sc = mm(cm[t0 : t0 + TQ, :], bm[0:ext, :], NT)
            tt = t0 + lax.broadcasted_iota(jnp.int32, (TQ, ext), 0)
            ss = lax.broadcasted_iota(jnp.int32, (TQ, ext), 1)
            keep = tt >= ss
            total = None
            for h in range(heads):
                wrow = GC[pl.ds(k * heads + h, 1), :][:, 0:ext]
                wcol = col[t0 : t0 + TQ, h * 128 : (h + 1) * 128]
                if ext > 128:
                    wcol = jnp.concatenate([wcol, wcol], axis=1)
                decay = jnp.where(keep, jnp.exp(jnp.minimum(wrow - wcol, 0.0)), 0.0)
                KH[t0 : t0 + TQ, h * BLOCK : h * BLOCK + ext] = (sc * decay).astype(BF16)
                mixing = mm(DYM[h * BLOCK + t0 : h * BLOCK + t0 + TQ, :], wx[0:ext, :], NT)
                part = mixing * decay
                total = part if total is None else total + part
            rows = pl.ds(pl.multiple_of(k * BLOCK + t0, TQ), TQ)
            MX[rows, 0:ext] = total.astype(BF16)
            if ext < BLOCK:
                MX[rows, ext:] = jnp.zeros((TQ, BLOCK - ext), BF16)
        YIN[blk(k), :] = mm(KH[...], WXM[...])
        acc = None
        for h in range(heads):
            part = mm(KH[:, h * BLOCK : (h + 1) * BLOCK], DYM[h * BLOCK : (h + 1) * BLOCK, :], TN)
            acc = part if acc is None else acc + part
        WGIN[blk(k), :] = acc
        return carry

    lax.fori_loop(nb - 2, nb, inside, 0)

    @pl.when(s > 0)
    def _():
        halo_x.wait_recv()
        halo_b.wait_recv()
        XF[0:8, :] = HXR[8:16, :].astype(F32)
        BCF[0:8, :] = HBR[8:16, :].astype(F32)

    conv_chunk(0, 0)
    dtot = TOT[0][0:1, :]
    for k in range(1, nb):
        dtot = dtot + TOT[k][0:1, :]
    tail0 = TOT[0][0:1, :]
    q1, q2, q3 = (p.astype(F32) for p in parts3(dtot))

    def edge_rows(v):
        v = jnp.where(edge, v, 0.0)
        v = jnp.where(rt == 8, q1, jnp.where(rt == 9, q2, jnp.where(rt == 10, q3, v)))
        return v.astype(BF16)

    CR[0, :, 0:W] = edge_rows(
        WX[0:16, :].astype(F32) * LEA[0:16, :] * jnp.exp(jnp.minimum(tail0 - dtot, 0.0))
    )
    CR[1, :, 0:W] = edge_rows(DYE[0:16, :].astype(F32))
    first = jnp.where(edge, BCP[0:16, :], jnp.zeros((16, W), BF16))
    CR[0, :, W:] = first[:, :N]
    CR[1, :, W:] = first[:, N:]
    for d in range(1, nseq):
        edge_copy(d).start()
    start0 = mm(first[:, :N], WL[0:16, :], TN)

    lax.fori_loop(0, nb - 2, inside, 0)

    def slopes(i, carry):
        r = blk(i, CH)
        BCS[r, :] = silu_slope(BCS[r, :])
        XS[r, :] = silu_slope(XS[r, :])
        GZ[r, :] = dout[r, :].astype(F32) * silu_slope(zg[r, :].astype(F32))
        return carry

    lax.fori_loop(0, T // CH, slopes, 0)

    def mixed(k, carry):
        r = blk(k)
        mx = MX[r, :]
        BS[r, :N] = mm(mx, BCP[r, N:], TN)
        BS[r, N:] = mm(mx, BCP[r, :N])
        return carry

    lax.fori_loop(0, nb, mixed, 0)

    for d in range(1, nseq):
        p, _ = other(d)
        send(EB.at[0], SLOT.at[p], s_st.at[d], r_st.at[p], at_seq(p)).wait_recv()
        send(CR.at[0], CSLOT.at[p], s_cr.at[d], r_cr.at[p], at_seq(p)).wait_recv()

    def fold(p, value):
        rows = CSLOT[p, :, 0:W]
        t3 = rows[8:16, :].astype(F32)
        dec = jnp.exp(-(t3[0:1, :] + t3[1:2, :] + t3[2:3, :]))
        late = mm(CSLOT[p, :, W:], rows, TN)
        return dec * value + (SLOT[p].astype(F32) + late)

    s_first = lax.fori_loop(0, s, fold, jnp.zeros((N, W), F32))
    g_last = lax.fori_loop(0, nseq - 1 - s, lambda i, v: fold(nseq - 1 - i, v), jnp.zeros((N, W), F32))
    SB[0] = s_first.astype(BF16)
    s_next = jnp.exp(-TOT[0][0:1, :]) * s_first + start0
    before = jnp.zeros((1, W), F32)
    for k in range(1, nb):
        SB[k] = (LS[k] + jnp.exp(-before) * s_next).astype(BF16)
        before = before + TOT[k][0:1, :]
    after = jnp.zeros((1, W), F32)
    for k in reversed(range(nb)):
        GB[k] = (NS[k] + jnp.exp(-after) * g_last).astype(BF16)
        after = after + TOT[k][0:1, :]

    def shared(k, carry):
        r = blk(k)
        BS[r, :N] = (BS[r, :N] + mm(WL[r, :], GB[k], NT)) * BCS[r, :N]
        BS[r, N:] = (BS[r, N:] + mm(DYE[r, :], SB[k], NT)) * BCS[r, N:]
        return carry

    shared(0, 0)
    HSB[0] = BS[0:8, :]
    halo_bs = send(HSB.at[0], HSB.at[1], s_sl.at[0], r_sl.at[0], at_seq(s - 1))

    @pl.when(s > 0)
    def _():
        halo_bs.start()

    lax.fori_loop(1, nb, shared, 0)

    def bc_adjoint(j, carry):
        u = BS[pl.ds(pl.multiple_of(j * own, 8), own + 8), :]
        out = cvb[0:1, :] * u[:own, :]
        for k in range(1, TAPS):
            out = out + cvb[k : k + 1, :] * pltpu.roll(u, own + 8 - k, 0)[:own, :]
        PR[j // nc, lax.rem(j, nc)] = out.astype(BF16)
        return carry

    pieces = [(0, nzy // 2), (nzy // 2, nzy - 1), (nzy - 1, nzy)]

    def a_copy(q):
        lo, hi = pieces[q]
        part = pl.ds(lo, hi - lo)
        return send(PR.at[part, 1 - c], RA.at[part], s_a.at[q], r_a.at[q], core_dev)

    def adjoint_piece(q):
        lax.fori_loop(pieces[q][0] * nc, pieces[q][1] * nc, bc_adjoint, 0)
        a_copy(q).start()

    def pair_sum(i, carry):
        ZS[i] = (PR[i, c].astype(F32) + RA[i].astype(F32)).astype(BF16)
        return carry

    def z_copy(d):
        t = other_zy(d)
        return send(ZS.at[t], RZ.at[m], s_z.at[d], r_z.at[m], at_zy(t))

    adjoint_piece(0)
    adjoint_piece(1)

    def tap_sums(slope, F, start, carry):
        n = slope.shape[0]
        v = F[pl.ds(pl.multiple_of(start, 8), n + 8), :]
        out = []
        for k in range(TAPS):
            moved = v[8:, :] if k == 0 else pltpu.roll(v, k, 0)[8:, :]
            out.append(carry[k] + (slope * moved).reshape(n // 8, 8, W).sum(axis=0))
        return tuple(out)

    def stack_taps(sums):
        rt8 = lax.broadcasted_iota(jnp.int32, (8, W), 0)
        out = jnp.zeros((8, W), F32)
        for k in range(TAPS):
            out = jnp.where(rt8 == k, jnp.sum(sums[k], axis=0, keepdims=True), out)
        return out

    zero4 = tuple(jnp.zeros((8, W), F32) for _ in range(TAPS))
    sums = lax.fori_loop(
        0, T // CH, lambda i, cr: tap_sums(BS[blk(i, CH), :], BCF, i * CH, cr), zero4
    )
    CBS[s] = stack_taps(sums)

    def seq_copy(buf, d, ss, rs):
        p, _ = other(d)
        return send(buf.at[s], buf.at[s], ss.at[d], rs.at[s], at_seq(p))

    def seq_wait(buf, ss, rs):
        for d in range(1, nseq):
            p, _ = other(d)
            send(buf.at[p], buf.at[p], ss.at[d], rs.at[p], at_seq(p)).wait_recv()

    for d in range(1, nseq):
        seq_copy(CBS, d, s_cb, r_cb).start()

    CW = 128
    lane1 = lax.broadcasted_iota(jnp.int32, (1, W), 1) // HEAD_DIM
    skip = by_head([d_s[h] for h in range(heads)], lane1)
    pick = (
        lax.broadcasted_iota(jnp.int32, (16, W), 0)
        == lax.broadcasted_iota(jnp.int32, (16, W), 1) // HEAD_DIM
    ).astype(F32).astype(BF16)

    def channels(i, carry):
        r = blk(i, CW)
        k = i // (BLOCK // CW)
        wg = WGIN[r, :] + LEA[r, :] * mm(BCP[r, :N], GB[k])
        xp = XP[r, :].astype(F32)
        slope = (DTE[r, :] * wg + skip * DY[r, :].astype(F32)) * XS[r, :]
        XSL[r, :] = slope
        prod = xp * wg
        hi = prod.astype(BF16)
        lo = (prod - hi.astype(F32)).astype(BF16)
        steps = mm(pick, hi, NT) + mm(pick, lo, NT)
        sg_o[:, pl.ds(pl.multiple_of(i * CW, CW), CW)] = steps[0:heads, :]
        return tap_sums(slope, XF, i * CW, carry)

    sums = channels(0, zero4)
    HSX[0] = XSL[0:8, :]
    halo_xs = send(HSX.at[0], HSX.at[1], s_sl.at[1], r_sl.at[1], at_seq(s - 1))

    @pl.when(s > 0)
    def _():
        halo_xs.start()

    for q in range(2):
        a_copy(q).wait_recv()
        lax.fori_loop(pieces[q][0], pieces[q][1], pair_sum, 0)
    for d in far_first:

        @pl.when(other_zy(d) < nzy - 1)
        def _():
            z_copy(d).start()

    sums = lax.fori_loop(1, 3, channels, sums)

    @pl.when(s < nseq - 1)
    def _():
        halo_bs.wait_recv()
        BS[T : T + 8, :] = HSB[1]

    @pl.when(s == nseq - 1)
    def _():
        BS[T : T + 8, :] = jnp.zeros((8, W), F32)

    adjoint_piece(2)
    sums = lax.fori_loop(3, 6, channels, sums)
    a_copy(2).wait_recv()
    pair_sum(nzy - 1, 0)

    @pl.when(m < nzy - 1)
    def _():
        z_copy(nzy - 1 - m).start()

    sums = lax.fori_loop(6, T // CW, channels, sums)
    CXS[s] = stack_taps(sums)
    for d in range(1, nseq):
        seq_copy(CXS, d, s_cx, r_cx).start()

    def total8(buf, n):
        out = buf[0]
        for p in range(1, n):
            out = out + buf[p]
        return out

    seq_wait(CBS, s_cb, r_cb)
    CBL[0] = total8(CBS, nseq)
    cc_copy = send(CBL.at[0], CBL.at[1], s_cc.at[0], r_cc.at[0], core_dev)
    cc_copy.start()

    def outputs(i, carry):
        r = blk(i, CH)
        k = i // (BLOCK // CH)
        y = YIN[r, :] + ENT[r, :] * mm(BCP[r, N:], SB[k]) + skip * XP[r, :].astype(F32)
        gg_o[r, :] = (GZ[r, :] * y).astype(BF16)
        return carry

    lax.fori_loop(0, T // CH // 2, outputs, 0)

    cc_copy.wait_recv()
    CBZ[m] = CBL[0] + CBL[1]

    def cz_copy(d):
        return send(CBZ.at[m], CBZ.at[m], s_cz.at[d], r_cz.at[m], at_zy(other_zy(d)))

    for d in far_first:
        cz_copy(d).start()

    lax.fori_loop(T // CH // 2, T // CH, outputs, 0)

    def x_adjoint(i, carry):
        r = blk(i, CH)
        u = XSL[pl.ds(pl.multiple_of(i * CH, 8), CH + 8), :]
        out = cvx[0:1, :] * u[:CH, :]
        for k in range(1, TAPS):
            out = out + cvx[k : k + 1, :] * pltpu.roll(u, CH + 8 - k, 0)[:CH, :]
        xg_o[r, :] = out.astype(BF16)
        return carry

    @pl.when(s < nseq - 1)
    def _():
        halo_xs.wait_recv()
        XSL[T : T + 8, :] = HSX[1]

    @pl.when(s == nseq - 1)
    def _():
        XSL[T : T + 8, :] = jnp.zeros((8, W), F32)

    lax.fori_loop(0, T // CH, x_adjoint, 0)

    seq_wait(CXS, s_cx, r_cx)
    cx_o[...] = total8(CXS, nseq)[0:TAPS, :]
    out = PR[m, c].astype(F32) + RA[m].astype(F32)
    for d in range(1, nzy):
        t = other_zy(d)
        send(ZS.at[t], RZ.at[t], s_z.at[d], r_z.at[t], at_zy(t)).wait_recv()
        out = out + RZ[t].astype(F32)
    bg_o[...] = out
    for d in range(1, nzy):
        t = other_zy(d)
        send(CBZ.at[t], CBZ.at[t], s_cz.at[d], r_cz.at[t], at_zy(t)).wait_recv()
    cb_o[...] = total8(CBZ, nzy)[0:TAPS, :]

    @pl.when(s < nseq - 1)
    def _():
        halo_x.wait_send()
        halo_b.wait_send()

    @pl.when(s > 0)
    def _():
        halo_bs.wait_send()
        halo_xs.wait_send()

    for d in range(1, nseq):
        state_copy(d).wait_send()
        edge_copy(d).wait_send()
        seq_copy(CBS, d, s_cb, r_cb).wait_send()
        seq_copy(CXS, d, s_cx, r_cx).wait_send()
    for q in range(3):
        a_copy(q).wait_send()
    for d in range(1, nzy):
        z_copy(d).wait_send()
        cz_copy(d).wait_send()
    cc_copy.wait_send()


def emit(*refs):
    held, outs, sem = refs[:6], refs[6:12], refs[12]
    copies = [pltpu.make_async_copy(a, b, sem.at[i]) for i, (a, b) in enumerate(zip(held, outs))]
    for copy in copies:
        copy.start()
    for copy in copies:
        copy.wait()


def local(dims, xraw, zgate, bcraw, dt, a_rate, d_skip, conv_x, conv_bc, dout):
    nx, nyh, nz, nyl, nc = dims
    nseq = nx * nyh
    nzy = nz * nyl
    T, W = xraw.shape
    nb = T // BLOCK
    heads = W // HEAD_DIM
    N = W // 2
    own = T // (nzy * nc)
    vm = lambda *shape: pltpu.VMEM(shape[:-1], shape[-1])
    full, half = vm(T, W, F32), vm(T, W, BF16)
    ext = vm(T + 8, W, F32)
    taps = vm(TAPS, W, F32)
    dma = lambda n: pltpu.SemaphoreType.DMA((n,))
    scratch = (
        [half, half, half, vm(heads, T, F32), taps, taps, half]
        + [ext, ext] + [full] * 8 + [ext, ext]
        + [half] * 5 + [half, vm(T, BLOCK, BF16)]
        + [vm(nb * heads, BLOCK, F32), vm(nb * heads, BLOCK, F32), vm(3 * nb * heads, BLOCK, BF16)]
        + [vm(nb, 8, W, F32)]
        + [vm(nb, N, W, F32)] * 4
        + [vm(nb, N, W, BF16)] * 2
        + [vm(2, N, W, BF16), vm(nseq, N, W, BF16)]
        + [vm(2, 16, W + N, BF16), vm(nseq, 16, W + N, BF16)]
        + [vm(BLOCK, heads * BLOCK, BF16), vm(heads * BLOCK, W, BF16), vm(heads * BLOCK, W, BF16)]
        + [vm(16, W, BF16)] * 2 + [vm(2, 8, W, F32)] * 2
        + [vm(nzy, nc, own, W, BF16), vm(nzy, own, W, BF16)]
        + [vm(nzy, own, W, BF16)] * 2
        + [vm(nseq, 8, W, F32)] * 2 + [vm(2, 8, W, F32), vm(nzy, 8, W, F32)]
        + [dma(7)] + [dma(2)] * 2 + [dma(nseq)] * 4 + [dma(2)] * 2 + [dma(3)] * 2 + [dma(nzy)] * 2
        + [dma(nseq)] * 4 + [dma(1)] * 2 + [dma(nzy)] * 2
    )
    vspec = pl.BlockSpec(memory_space=pltpu.VMEM)
    sspec = pl.BlockSpec(memory_space=pltpu.SMEM)
    hspec = pl.BlockSpec(memory_space=pltpu.HBM)
    shapes = [
        ((T, W), BF16), ((T, W), BF16), ((heads, T), F32), ((own, W), F32), ((TAPS, W), F32), ((TAPS, W), F32),
    ]
    held = pl.pallas_call(
        functools.partial(kernel, dims, T, W),
        name="ssd_backward",
        out_shape=tuple(pltpu.VMEM(*sh) for sh in shapes),
        in_specs=[hspec, hspec, hspec, hspec, sspec, sspec, hspec, hspec, hspec],
        out_specs=tuple([vspec] * 6),
        scratch_shapes=scratch,
        compiler_params=pltpu.CompilerParams(
            collective_id=0, has_side_effects=True, vmem_limit_bytes=60 * 1024 * 1024
        ),
    )(xraw, zgate, bcraw, dt, a_rate, d_skip, conv_x, conv_bc, dout)
    return pl.pallas_call(
        emit,
        name="emit",
        out_shape=tuple(jax.ShapeDtypeStruct(*sh) for sh in shapes),
        in_specs=[vspec] * 6,
        out_specs=tuple([hspec] * 6),
        scratch_shapes=[dma(6)],
        compiler_params=pltpu.CompilerParams(vmem_limit_bytes=4 * 1024 * 1024),
    )(*held)


def over_mesh(torus):
    placed = (
        P(SEQ, HEAD), P(SEQ, HEAD), P(SEQ, None), P(HEAD, SEQ), P(HEAD), P(HEAD),
        P(None, HEAD), P(), P(SEQ, HEAD),
    )
    return jax.shard_map(
        functools.partial(local, tuple(torus.devices.shape)),
        mesh=torus,
        in_specs=placed,
        out_specs=(P(SEQ, HEAD), P(SEQ, HEAD), P(HEAD, SEQ), P(SEQ_HEAD, None), P(None, HEAD), P()),
        check_vma=False,
    )


def solution(mesh):
    return over_mesh(Mesh(mesh.devices.reshape(4, 2, 8, 2, 2), SEQ_HEAD))
```

time: 49.9 us -> 42.8 us (0.86); the launches traced: 49.1 us -> 42.7 us
  local copies, waits for them, and re-layouts: 5.43 us -> 0 us
  Pallas kernels: 43 us -> 42 us
    unnamed x16 -> x0, local copies, waits for them, and re-layouts: 5.43 us -> none
    pallas_call x1, Pallas kernels: 43 us -> 41 us  [local(): pl.pallas_call(functools.partial(kernel, dims, T, W), name='ssd_backward'...]
    pallas_call x0 -> x1, Pallas kernels: none -> 1.03 us  [local(): pl.pallas_call(emit, name='emit', out_shape=tuple((jax.ShapeDtypeStruct(*...]
where the time goes in v2:
time: 42.8 us; the launch traced here: 42.7 us
  Pallas kernels  42 us (98%)
  between operations  0.64 us (1%)
    pallas_call x1, Pallas kernels, local(): pl.pallas_call(functools.partial(kernel, dims, T, W), name='ssd_backward'...  41 us
    pallas_call x1, Pallas kernels, local(): pl.pallas_call(emit, name='emit', out_shape=tuple((jax.ShapeDtypeStruct(*...  1.03 us

profile of v2, /device:TPU:1, one launch (start us, length us, event | category | flops | bytes accessed | tf_op | source)
XLA Modules:
  0.0 42.7 jit_solution(5425096312917532147)
XLA Ops:
  0.6 41.0 %ssd_backward.1 = (bf16[1024,256]{1,0:T(8,128)(2,1)S(1)}, bf16[1024,256]{1,0:T(8,128)(2,1)S(1)}, f32[4,1024]{1,0:T(4,128)S(1)}, f32[32,256]{1,0:T(8,128)S(1)}, f...) custom-call(bf16[1024,256]{1,0:T(8,128)(2,1)} %xraw_h.1, bf16[1024,256]{1,0:T(8,128)(2,1)} %zg_h.1, bf16[1024,256]{1,0:T(8,128)(2,1)} %bcr_h.1, ...), custom_call_target="tpu_custom_call" | custom-call | tf_op jit(solution)/shard_map/ssd_backward/pallas_call | solution.py:641
  41.6 1.0 %emit.1 = (bf16[1024,256]{1,0:T(8,128)(2,1)}, bf16[1024,256]{1,0:T(8,128)(2,1)}, f32[4,1024]{1,0:T(4,128)}, f32[32,256]{1,0:T(8,128)}, f32[4,256]{1,0:T(4,128)}, /*index=5*/f32[4,256]{1,0:T(4,128)}) custom-call(bf16[1024,256]{1,0:T(8,128)(2,1)S(1)} %get-tuple-element.12.refs_0_, bf16[1024,256]{1,0:T(8,128)(2,1)S(1)} %get-tuple-element.13.refs_1_, ...), custom_call_target="tpu_custom_call" | custom-call | tf_op jit(solution)/shard_map/emit/pallas_call | solution.py:652

commit v3 on v2

--- a/solution.py
+++ b/solution.py
@@ -42,6 +42,28 @@
     return q * (1.0 + v * (1.0 - q))
 
 
+def loop(lo, hi, body, carry=0, unroll=1):
+    if unroll >= hi - lo:
+        for i in range(lo, hi):
+            carry = body(i, carry)
+        return carry
+
+    def some(j, carry):
+        for u in range(unroll):
+            carry = body(lo + j * unroll + u, carry)
+        return carry
+
+    return lax.fori_loop(0, (hi - lo) // unroll, some, carry)
+
+
+def part(k, n):
+    return pl.ds(k * n if isinstance(k, int) else pl.multiple_of(k * n, n), n)
+
+
+def window(start, n):
+    return pl.ds(start if isinstance(start, int) else pl.multiple_of(start, 8), n)
+
+
 def by_head(scalars, lanes):
     out = jnp.full(lanes.shape, scalars[3], F32)
     for h in (2, 1, 0):
@@ -54,13 +76,13 @@
     xraw_h, zg_h, bcr_h, dt_h, a_s, d_s, cvx_h, cvb_h, dout_h,
     xg_o, gg_o, sg_o, bg_o, cx_o, cb_o,
     xraw, zg, bcr, dt, cvx, cvb, dout,
-    XF, BCF, XS, BCS, GZ, DTE, ENT, LEA, YIN, WGIN, XSL, BS,
+    XF, BCF, XS, BCS, DTE, ENT, LEA, YIN, WGIN, XSL, BS,
     XP, WX, WL, DY, DYE, BCP, MX,
-    GC, DC, WP, TOT, EK, BK, LS, NS, SB, GB, EB, SLOT, CR, CSLOT,
+    GC, DC, WP, TOT, LS, NS, SB, GB, EB, SLOT, CR, CSLOT, FS, DEC,
     KH, WXM, DYM, HXR, HBR, HSX, HSB,
-    PR, RA, ZS, RZ, CXS, CBS, CBL, CBZ,
+    PR, RA, ZS, RZ, CXS, CBS, CBZ,
     s_in, s_h, r_h, s_st, r_st, s_cr, r_cr, s_sl, r_sl, s_a, r_a, s_z, r_z,
-    s_cx, r_cx, s_cb, r_cb, s_cc, r_cc, s_cz, r_cz,
+    s_cx, r_cx, s_cb, r_cb, s_cz, r_cz,
 ):
     nx, nyh, nz, nyl, nc = dims
     nseq = nx * nyh
@@ -106,6 +128,8 @@
     for d in far_first:
         greet(at_zy(other_zy(d)))
     greet(core_dev)
+    for d in range(1, nseq):
+        greet({**at_seq(other(d)[0]), **core_dev})
 
     loads = [
         pltpu.make_async_copy(a, b, s_in.at[i])
@@ -138,7 +162,7 @@
     WP[...] = wp
 
     def blk(k, n=BLOCK):
-        return pl.ds(pl.multiple_of(k * n, n), n)
+        return part(k, n)
 
     def expand(k, carry):
         hot = ((rr // heads == k) & (lax.rem(rr, heads) == ll)).astype(F32).astype(BF16)
@@ -150,7 +174,7 @@
         DTE[blk(k), :] = mm(dp, hot, TN)
         return carry
 
-    lax.fori_loop(0, nb, expand, 0)
+    loop(0, nb, expand, 0, 2)
 
     CH = 64
     N = W // 2
@@ -166,28 +190,29 @@
         dy = (dout[r, :].astype(F32) * (zv * sigmoid(zv))).astype(BF16)
         DY[r, :] = dy
         DYE[r, :] = (dy.astype(F32) * ENT[r, :]).astype(BF16)
-        shifted = pl.ds(pl.multiple_of(8 + i * CH, 8), CH)
+        shifted = window(8 + i * CH, CH)
         XF[shifted, :] = xraw[r, :].astype(F32)
         BCF[shifted, :] = bcr[r, :].astype(F32)
         return carry
 
-    lax.fori_loop(0, T // CH, gates, 0)
-
-    def conv_chunk(i, carry):
+    loop(0, T // CH, gates, 0, 2)
+
+    def pre(F, taps, i):
+        v = F[window(i * CH, CH + 8), :]
+        out = taps[0:1, :] * v[8:, :]
+        for k in range(1, TAPS):
+            out = out + taps[k : k + 1, :] * pltpu.roll(v, k, 0)[8:, :]
+        return out
+
+    def conv_bc_chunk(i, carry):
+        v = pre(BCF, cvb, i)
+        BCP[blk(i, CH), :] = (v * sigmoid(v)).astype(BF16)
+        BCS[blk(i, CH), :] = v
+        return carry
+
+    def conv_x_chunk(i, carry):
         r = blk(i, CH)
-        ext = pl.ds(pl.multiple_of(i * CH, 8), CH + 8)
-
-        def pre(F, taps):
-            v = F[ext, :]
-            out = taps[0:1, :] * v[8:, :]
-            for k in range(1, TAPS):
-                out = out + taps[k : k + 1, :] * pltpu.roll(v, k, 0)[8:, :]
-            return out
-
-        v = pre(BCF, cvb)
-        BCP[r, :] = (v * sigmoid(v)).astype(BF16)
-        BCS[r, :] = v
-        v = pre(XF, cvx)
+        v = pre(XF, cvx, i)
         post = (v * sigmoid(v)).astype(BF16)
         XP[r, :] = post
         XS[r, :] = v
@@ -196,62 +221,67 @@
         WL[r, :] = (wx.astype(F32) * LEA[r, :]).astype(BF16)
         return carry
 
-    def block_ends(k, carry):
-        EK[k] = mm(BCP[blk(k), :N], WL[blk(k), :], TN)
-        BK[k] = mm(BCP[blk(k), N:], DYE[blk(k), :], TN)
-        return carry
-
-    lax.fori_loop(0, T // CH, conv_chunk, 0)
+    loop(0, T // CH, conv_bc_chunk, 0, 2)
     rt = lax.broadcasted_iota(jnp.int32, (16, W), 0)
     edge = rt < TAPS - 1
     BCP[0:16, :] = jnp.where(edge, jnp.zeros((16, W), BF16), BCP[0:16, :])
-    lax.fori_loop(0, nb, block_ends, 0)
-
+
+    grads = [mm(BCP[blk(k), N:], DYE[blk(k), :], TN) for k in range(nb)]
+    grad = jnp.zeros((N, W), F32)
+    for k in reversed(range(nb)):
+        NS[k] = grad
+        grad = jnp.exp(-TOT[k][0:1, :]) * grad + grads[k]
+    EB[1] = grad.astype(BF16)
+
+    pl.semaphore_wait(barrier, nseq * nc - 1 + nzy - 1)
+
+    halo_x = send(xraw.at[T - 16 :], HXR, s_h.at[0], r_h.at[0], at_seq(s + 1))
+    halo_b = send(bcr.at[T - 16 :], HBR, s_h.at[1], r_h.at[1], at_seq(s + 1))
+
+    @pl.when(s < nseq - 1)
+    def _():
+        halo_x.start()
+        halo_b.start()
+
+    def state_copy(d):
+        p, wrapped = other(d)
+        return send(EB.at[wrapped], SLOT.at[s], s_st.at[d], r_st.at[s], at_seq(p))
+
+    def edge_copy(d):
+        p, wrapped = other(d)
+        return send(CR.at[wrapped], CSLOT.at[s], s_cr.at[d], r_cr.at[s], at_seq(p))
+
+    for d in sorted(range(1, nseq), key=lambda d: -min(d, nseq - d)):
+
+        @pl.when(s + d >= nseq)
+        def _():
+            state_copy(d).start()
+
+    loop(0, T // CH, conv_x_chunk, 0, 2)
+    ends = [mm(BCP[blk(k), :N], WL[blk(k), :], TN) for k in range(nb)]
     state = jnp.zeros((N, W), F32)
     for k in range(nb):
         LS[k] = state
-        state = jnp.exp(-TOT[k][0:1, :]) * state + EK[k]
+        state = jnp.exp(-TOT[k][0:1, :]) * state + ends[k]
     EB[0] = state.astype(BF16)
-    grad = jnp.zeros((N, W), F32)
-    for k in reversed(range(nb)):
-        NS[k] = grad
-        grad = jnp.exp(-TOT[k][0:1, :]) * grad + BK[k]
-    EB[1] = grad.astype(BF16)
-
-    pl.semaphore_wait(barrier, nseq - 1 + nzy - 1 + 1)
-
-    halo_x = send(xraw.at[T - 16 :], HXR, s_h.at[0], r_h.at[0], at_seq(s + 1))
-    halo_b = send(bcr.at[T - 16 :], HBR, s_h.at[1], r_h.at[1], at_seq(s + 1))
-
-    @pl.when(s < nseq - 1)
-    def _():
-        halo_x.start()
-        halo_b.start()
-
-    def state_copy(d):
-        p, wrapped = other(d)
-        return send(EB.at[wrapped], SLOT.at[s], s_st.at[d], r_st.at[s], at_seq(p))
-
-    def edge_copy(d):
-        p, wrapped = other(d)
-        return send(CR.at[wrapped], CSLOT.at[s], s_cr.at[d], r_cr.at[s], at_seq(p))
-
-    for d in range(1, nseq):
-        state_copy(d).start()
+    for d in sorted(range(1, nseq), key=lambda d: -min(d, nseq - d)):
+
+        @pl.when(s + d < nseq)
+        def _():
+            state_copy(d).start()
 
     lane_h = lax.broadcasted_iota(jnp.int32, (BLOCK, W), 1) // HEAD_DIM
     r512 = lax.rem(lax.broadcasted_iota(jnp.int32, (3 * n16, heads * 128), 0), n16)
     l512 = lax.broadcasted_iota(jnp.int32, (3 * n16, heads * 128), 1) // 128
     for h in range(heads):
-        KH[0:128, h * BLOCK + 128 : (h + 1) * BLOCK] = jnp.zeros((128, 128), BF16)
+        KH[:, 0:128, h * BLOCK + 128 : (h + 1) * BLOCK] = jnp.zeros((nb, 128, 128), BF16)
     TQ = 64
 
     def inside(k, carry):
         bm, cm = BCP[blk(k), :N], BCP[blk(k), N:]
         wx, dy = WX[blk(k), :], DY[blk(k), :]
         for h in range(heads):
-            WXM[h * BLOCK : (h + 1) * BLOCK, :] = jnp.where(lane_h == h, wx, jnp.zeros_like(wx))
-            DYM[h * BLOCK : (h + 1) * BLOCK, :] = jnp.where(lane_h == h, dy, jnp.zeros_like(dy))
+            DYM[k, h * BLOCK : (h + 1) * BLOCK, :] = jnp.where(lane_h == h, dy, jnp.zeros_like(dy))
         hot = ((r512 // heads == k) & (lax.rem(r512, heads) == l512)).astype(F32).astype(BF16)
         col = mm(WP[...], hot, TN)
         for t0 in range(0, BLOCK, TQ):
@@ -267,23 +297,31 @@
                 if ext > 128:
                     wcol = jnp.concatenate([wcol, wcol], axis=1)
                 decay = jnp.where(keep, jnp.exp(jnp.minimum(wrow - wcol, 0.0)), 0.0)
-                KH[t0 : t0 + TQ, h * BLOCK : h * BLOCK + ext] = (sc * decay).astype(BF16)
-                mixing = mm(DYM[h * BLOCK + t0 : h * BLOCK + t0 + TQ, :], wx[0:ext, :], NT)
+                KH[k, t0 : t0 + TQ, h * BLOCK : h * BLOCK + ext] = (sc * decay).astype(BF16)
+                mixing = mm(DYM[k, h * BLOCK + t0 : h * BLOCK + t0 + TQ, :], wx[0:ext, :], NT)
                 part = mixing * decay
                 total = part if total is None else total + part
-            rows = pl.ds(pl.multiple_of(k * BLOCK + t0, TQ), TQ)
+            rows = window(k * BLOCK + t0, TQ)
             MX[rows, 0:ext] = total.astype(BF16)
             if ext < BLOCK:
                 MX[rows, ext:] = jnp.zeros((TQ, BLOCK - ext), BF16)
-        YIN[blk(k), :] = mm(KH[...], WXM[...])
+        return carry
+
+    def inner(k, carry):
+        wx = WX[blk(k), :]
+        for h in range(heads):
+            WXM[h * BLOCK : (h + 1) * BLOCK, :] = jnp.where(lane_h == h, wx, jnp.zeros_like(wx))
         acc = None
         for h in range(heads):
-            part = mm(KH[:, h * BLOCK : (h + 1) * BLOCK], DYM[h * BLOCK : (h + 1) * BLOCK, :], TN)
-            acc = part if acc is None else acc + part
+            part_h = mm(
+                KH[k, :, h * BLOCK : (h + 1) * BLOCK], DYM[k, h * BLOCK : (h + 1) * BLOCK, :], TN
+            )
+            acc = part_h if acc is None else acc + part_h
         WGIN[blk(k), :] = acc
-        return carry
-
-    lax.fori_loop(nb - 2, nb, inside, 0)
+        YIN[blk(k), :] = mm(KH[k], WXM[...])
+        return carry
+
+    loop(nb - 1, nb, inside, 0, 1)
 
     @pl.when(s > 0)
     def _():
@@ -292,7 +330,8 @@
         XF[0:8, :] = HXR[8:16, :].astype(F32)
         BCF[0:8, :] = HBR[8:16, :].astype(F32)
 
-    conv_chunk(0, 0)
+    conv_bc_chunk(0, 0)
+    conv_x_chunk(0, 0)
     dtot = TOT[0][0:1, :]
     for k in range(1, nb):
         dtot = dtot + TOT[k][0:1, :]
@@ -315,40 +354,36 @@
         edge_copy(d).start()
     start0 = mm(first[:, :N], WL[0:16, :], TN)
 
-    lax.fori_loop(0, nb - 2, inside, 0)
-
-    def slopes(i, carry):
-        r = blk(i, CH)
-        BCS[r, :] = silu_slope(BCS[r, :])
-        XS[r, :] = silu_slope(XS[r, :])
-        GZ[r, :] = dout[r, :].astype(F32) * silu_slope(zg[r, :].astype(F32))
-        return carry
-
-    lax.fori_loop(0, T // CH, slopes, 0)
+    loop(0, nb - 1, inside, 0, 1)
 
     def mixed(k, carry):
         r = blk(k)
         mx = MX[r, :]
         BS[r, :N] = mm(mx, BCP[r, N:], TN)
         BS[r, N:] = mm(mx, BCP[r, :N])
-        return carry
-
-    lax.fori_loop(0, nb, mixed, 0)
+        BCS[r, :] = silu_slope(BCS[r, :])
+        return carry
+
+    loop(0, nb, mixed, 0, 4)
 
     for d in range(1, nseq):
         p, _ = other(d)
         send(EB.at[0], SLOT.at[p], s_st.at[d], r_st.at[p], at_seq(p)).wait_recv()
         send(CR.at[0], CSLOT.at[p], s_cr.at[d], r_cr.at[p], at_seq(p)).wait_recv()
 
-    def fold(p, value):
+    for d in range(1, nseq):
+        p, _ = other(d)
         rows = CSLOT[p, :, 0:W]
         t3 = rows[8:16, :].astype(F32)
-        dec = jnp.exp(-(t3[0:1, :] + t3[1:2, :] + t3[2:3, :]))
-        late = mm(CSLOT[p, :, W:], rows, TN)
-        return dec * value + (SLOT[p].astype(F32) + late)
-
-    s_first = lax.fori_loop(0, s, fold, jnp.zeros((N, W), F32))
-    g_last = lax.fori_loop(0, nseq - 1 - s, lambda i, v: fold(nseq - 1 - i, v), jnp.zeros((N, W), F32))
+        DEC[p] = jnp.broadcast_to(jnp.exp(-(t3[0:1, :] + t3[1:2, :] + t3[2:3, :])), (8, W))
+        FS[p] = SLOT[p].astype(F32) + mm(CSLOT[p, :, W:], rows, TN)
+
+    def fold(p, value):
+        return DEC[p][0:1, :] * value + FS[p]
+
+    zero_state = jnp.zeros((N, W), F32)
+    s_first = lax.fori_loop(0, s, fold, zero_state)
+    g_last = lax.fori_loop(0, nseq - 1 - s, lambda i, v: fold(nseq - 1 - i, v), zero_state)
     SB[0] = s_first.astype(BF16)
     s_next = jnp.exp(-TOT[0][0:1, :]) * s_first + start0
     before = jnp.zeros((1, W), F32)
@@ -374,10 +409,10 @@
     def _():
         halo_bs.start()
 
-    lax.fori_loop(1, nb, shared, 0)
+    loop(1, nb, shared, 0, 3)
 
     def bc_adjoint(j, carry):
-        u = BS[pl.ds(pl.multiple_of(j * own, 8), own + 8), :]
+        u = BS[window(j * own, own + 8), :]
         out = cvb[0:1, :] * u[:own, :]
         for k in range(1, TAPS):
             out = out + cvb[k : k + 1, :] * pltpu.roll(u, own + 8 - k, 0)[:own, :]
@@ -392,7 +427,7 @@
         return send(PR.at[part, 1 - c], RA.at[part], s_a.at[q], r_a.at[q], core_dev)
 
     def adjoint_piece(q):
-        lax.fori_loop(pieces[q][0] * nc, pieces[q][1] * nc, bc_adjoint, 0)
+        loop(pieces[q][0] * nc, pieces[q][1] * nc, bc_adjoint, 0, 2)
         a_copy(q).start()
 
     def pair_sum(i, carry):
@@ -403,12 +438,9 @@
         t = other_zy(d)
         return send(ZS.at[t], RZ.at[m], s_z.at[d], r_z.at[m], at_zy(t))
 
-    adjoint_piece(0)
-    adjoint_piece(1)
-
     def tap_sums(slope, F, start, carry):
         n = slope.shape[0]
-        v = F[pl.ds(pl.multiple_of(start, 8), n + 8), :]
+        v = F[window(start, n + 8), :]
         out = []
         for k in range(TAPS):
             moved = v[8:, :] if k == 0 else pltpu.roll(v, k, 0)[8:, :]
@@ -416,17 +448,26 @@
         return tuple(out)
 
     def stack_taps(sums):
-        rt8 = lax.broadcasted_iota(jnp.int32, (8, W), 0)
-        out = jnp.zeros((8, W), F32)
+        rt4 = lax.broadcasted_iota(jnp.int32, (TAPS, W), 0)
+        out = jnp.zeros((TAPS, W), F32)
         for k in range(TAPS):
-            out = jnp.where(rt8 == k, jnp.sum(sums[k], axis=0, keepdims=True), out)
+            out = jnp.where(rt4 == k, jnp.sum(sums[k], axis=0, keepdims=True), out)
         return out
 
     zero4 = tuple(jnp.zeros((8, W), F32) for _ in range(TAPS))
-    sums = lax.fori_loop(
-        0, T // CH, lambda i, cr: tap_sums(BS[blk(i, CH), :], BCF, i * CH, cr), zero4
+    sums = loop(
+        0, T // CH, lambda i, cr: tap_sums(BS[blk(i, CH), :], BCF, i * CH, cr), zero4, 2
     )
-    CBS[s] = stack_taps(sums)
+    CBZ[m] = stack_taps(sums)
+
+    def cz_copy(d):
+        return send(CBZ.at[m], CBZ.at[m], s_cz.at[d], r_cz.at[m], at_zy(other_zy(d)))
+
+    for d in far_first:
+        cz_copy(d).start()
+
+    adjoint_piece(0)
+    adjoint_piece(1)
 
     def seq_copy(buf, d, ss, rs):
         p, _ = other(d)
@@ -436,9 +477,6 @@
         for d in range(1, nseq):
             p, _ = other(d)
             send(buf.at[p], buf.at[p], ss.at[d], rs.at[p], at_seq(p)).wait_recv()
-
-    for d in range(1, nseq):
-        seq_copy(CBS, d, s_cb, r_cb).start()
 
     CW = 128
     lane1 = lax.broadcasted_iota(jnp.int32, (1, W), 1) // HEAD_DIM
@@ -453,16 +491,22 @@
         k = i // (BLOCK // CW)
         wg = WGIN[r, :] + LEA[r, :] * mm(BCP[r, :N], GB[k])
         xp = XP[r, :].astype(F32)
-        slope = (DTE[r, :] * wg + skip * DY[r, :].astype(F32)) * XS[r, :]
+        slope = (DTE[r, :] * wg + skip * DY[r, :].astype(F32)) * silu_slope(XS[r, :])
         XSL[r, :] = slope
         prod = xp * wg
         hi = prod.astype(BF16)
         lo = (prod - hi.astype(F32)).astype(BF16)
         steps = mm(pick, hi, NT) + mm(pick, lo, NT)
-        sg_o[:, pl.ds(pl.multiple_of(i * CW, CW), CW)] = steps[0:heads, :]
+        sg_o[:, part(i, CW)] = steps[0:heads, :]
         return tap_sums(slope, XF, i * CW, carry)
 
-    sums = channels(0, zero4)
+    halves = BLOCK // CW
+
+    def block_channels(k, sums):
+        inner(k, 0)
+        return loop(k * halves, (k + 1) * halves, channels, sums, halves)
+
+    sums = block_channels(0, zero4)
     HSX[0] = XSL[0:8, :]
     halo_xs = send(HSX.at[0], HSX.at[1], s_sl.at[1], r_sl.at[1], at_seq(s - 1))
 
@@ -472,15 +516,13 @@
 
     for q in range(2):
         a_copy(q).wait_recv()
-        lax.fori_loop(pieces[q][0], pieces[q][1], pair_sum, 0)
+        loop(pieces[q][0], pieces[q][1], pair_sum, 0, nzy)
     for d in far_first:
 
         @pl.when(other_zy(d) < nzy - 1)
         def _():
             z_copy(d).start()
 
-    sums = lax.fori_loop(1, 3, channels, sums)
-
     @pl.when(s < nseq - 1)
     def _():
         halo_bs.wait_recv()
@@ -491,7 +533,7 @@
         BS[T : T + 8, :] = jnp.zeros((8, W), F32)
 
     adjoint_piece(2)
-    sums = lax.fori_loop(3, 6, channels, sums)
+    sums = block_channels(1, sums)
     a_copy(2).wait_recv()
     pair_sum(nzy - 1, 0)
 
@@ -499,45 +541,45 @@
     def _():
         z_copy(nzy - 1 - m).start()
 
-    sums = lax.fori_loop(6, T // CW, channels, sums)
+    sums = block_channels(2, sums)
+    sums = block_channels(3, sums)
     CXS[s] = stack_taps(sums)
     for d in range(1, nseq):
         seq_copy(CXS, d, s_cx, r_cx).start()
 
-    def total8(buf, n):
+    def total(buf, n):
         out = buf[0]
         for p in range(1, n):
             out = out + buf[p]
         return out
 
-    seq_wait(CBS, s_cb, r_cb)
-    CBL[0] = total8(CBS, nseq)
-    cc_copy = send(CBL.at[0], CBL.at[1], s_cc.at[0], r_cc.at[0], core_dev)
-    cc_copy.start()
+    for d in range(1, nzy):
+        t = other_zy(d)
+        send(CBZ.at[t], CBZ.at[t], s_cz.at[d], r_cz.at[t], at_zy(t)).wait_recv()
+    mine = s * nc + c
+    CBS[mine] = total(CBZ, nzy)
+
+    def sc_copy(d):
+        p, _ = other(d // 2)
+        dev = at_seq(p) if d % 2 == 0 else {**at_seq(p), **core_dev}
+        return send(CBS.at[mine], CBS.at[mine], s_cb.at[d], r_cb.at[mine], dev)
+
+    for d in range(1, nseq * nc):
+        sc_copy(d).start()
 
     def outputs(i, carry):
         r = blk(i, CH)
         k = i // (BLOCK // CH)
         y = YIN[r, :] + ENT[r, :] * mm(BCP[r, N:], SB[k]) + skip * XP[r, :].astype(F32)
-        gg_o[r, :] = (GZ[r, :] * y).astype(BF16)
-        return carry
-
-    lax.fori_loop(0, T // CH // 2, outputs, 0)
-
-    cc_copy.wait_recv()
-    CBZ[m] = CBL[0] + CBL[1]
-
-    def cz_copy(d):
-        return send(CBZ.at[m], CBZ.at[m], s_cz.at[d], r_cz.at[m], at_zy(other_zy(d)))
-
-    for d in far_first:
-        cz_copy(d).start()
-
-    lax.fori_loop(T // CH // 2, T // CH, outputs, 0)
+        gate = dout[r, :].astype(F32) * silu_slope(zg[r, :].astype(F32))
+        gg_o[r, :] = (gate * y).astype(BF16)
+        return carry
+
+    loop(0, T // CH, outputs, 0, 4)
 
     def x_adjoint(i, carry):
         r = blk(i, CH)
-        u = XSL[pl.ds(pl.multiple_of(i * CH, 8), CH + 8), :]
+        u = XSL[window(i * CH, CH + 8), :]
         out = cvx[0:1, :] * u[:CH, :]
         for k in range(1, TAPS):
             out = out + cvx[k : k + 1, :] * pltpu.roll(u, CH + 8 - k, 0)[:CH, :]
@@ -553,20 +595,21 @@
     def _():
         XSL[T : T + 8, :] = jnp.zeros((8, W), F32)
 
-    lax.fori_loop(0, T // CH, x_adjoint, 0)
+    loop(0, T // CH, x_adjoint, 0, 2)
 
     seq_wait(CXS, s_cx, r_cx)
-    cx_o[...] = total8(CXS, nseq)[0:TAPS, :]
+    cx_o[...] = total(CXS, nseq)
     out = PR[m, c].astype(F32) + RA[m].astype(F32)
     for d in range(1, nzy):
         t = other_zy(d)
         send(ZS.at[t], RZ.at[t], s_z.at[d], r_z.at[t], at_zy(t)).wait_recv()
         out = out + RZ[t].astype(F32)
     bg_o[...] = out
-    for d in range(1, nzy):
-        t = other_zy(d)
-        send(CBZ.at[t], CBZ.at[t], s_cz.at[d], r_cz.at[t], at_zy(t)).wait_recv()
-    cb_o[...] = total8(CBZ, nzy)[0:TAPS, :]
+    for d in range(1, nseq * nc):
+        p, _ = other(d // 2)
+        slot = p * nc + (c if d % 2 == 0 else 1 - c)
+        send(CBS.at[slot], CBS.at[slot], s_cb.at[d], r_cb.at[slot], core_dev).wait_recv()
+    cb_o[...] = total(CBS, nseq * nc)
 
     @pl.when(s < nseq - 1)
     def _():
@@ -581,14 +624,14 @@
     for d in range(1, nseq):
         state_copy(d).wait_send()
         edge_copy(d).wait_send()
-        seq_copy(CBS, d, s_cb, r_cb).wait_send()
         seq_copy(CXS, d, s_cx, r_cx).wait_send()
     for q in range(3):
         a_copy(q).wait_send()
     for d in range(1, nzy):
         z_copy(d).wait_send()
         cz_copy(d).wait_send()
-    cc_copy.wait_send()
+    for d in range(1, nseq * nc):
+        sc_copy(d).wait_send()
 
 
 def emit(*refs):
@@ -616,21 +659,23 @@
     dma = lambda n: pltpu.SemaphoreType.DMA((n,))
     scratch = (
         [half, half, half, vm(heads, T, F32), taps, taps, half]
-        + [ext, ext] + [full] * 8 + [ext, ext]
+        + [ext, ext] + [full] * 7 + [ext, ext]
         + [half] * 5 + [half, vm(T, BLOCK, BF16)]
         + [vm(nb * heads, BLOCK, F32), vm(nb * heads, BLOCK, F32), vm(3 * nb * heads, BLOCK, BF16)]
         + [vm(nb, 8, W, F32)]
-        + [vm(nb, N, W, F32)] * 4
+        + [vm(nb, N, W, F32)] * 2
         + [vm(nb, N, W, BF16)] * 2
         + [vm(2, N, W, BF16), vm(nseq, N, W, BF16)]
         + [vm(2, 16, W + N, BF16), vm(nseq, 16, W + N, BF16)]
-        + [vm(BLOCK, heads * BLOCK, BF16), vm(heads * BLOCK, W, BF16), vm(heads * BLOCK, W, BF16)]
+        + [vm(nseq, N, W, F32), vm(nseq, 8, W, F32)]
+        + [vm(nb, BLOCK, heads * BLOCK, BF16), vm(heads * BLOCK, W, BF16)]
+        + [vm(nb, heads * BLOCK, W, BF16)]
         + [vm(16, W, BF16)] * 2 + [vm(2, 8, W, F32)] * 2
         + [vm(nzy, nc, own, W, BF16), vm(nzy, own, W, BF16)]
         + [vm(nzy, own, W, BF16)] * 2
-        + [vm(nseq, 8, W, F32)] * 2 + [vm(2, 8, W, F32), vm(nzy, 8, W, F32)]
+        + [vm(nseq, TAPS, W, F32), vm(nseq * nc, TAPS, W, F32), vm(nzy, TAPS, W, F32)]
         + [dma(7)] + [dma(2)] * 2 + [dma(nseq)] * 4 + [dma(2)] * 2 + [dma(3)] * 2 + [dma(nzy)] * 2
-        + [dma(nseq)] * 4 + [dma(1)] * 2 + [dma(nzy)] * 2
+        + [dma(nseq)] * 2 + [dma(nseq * nc)] * 2 + [dma(nzy)] * 2
     )
     vspec = pl.BlockSpec(memory_space=pltpu.VMEM)
     sspec = pl.BlockSpec(memory_space=pltpu.SMEM)

time: 42.8 us -> 39.6 us (0.925)
  Pallas kernels: 42 us -> 38.8 us
    pallas_call x1, Pallas kernels: 41 us -> 37.8 us  [local(): pl.pallas_call(functools.partial(kernel, dims, T, W), name='ssd_backward'...]
where the time goes in v3:
time: 39.6 us; the launch traced here: 39.4 us
  Pallas kernels  38.8 us (98%)
  between operations  0.64 us (2%)
    pallas_call x1, Pallas kernels, local(): pl.pallas_call(functools.partial(kernel, dims, T, W), name='ssd_backward'...  37.8 us
    pallas_call x1, Pallas kernels, local(): pl.pallas_call(emit, name='emit', out_shape=tuple((jax.ShapeDtypeStruct(*...  1.03 us

profile of v3, /device:TPU:1, one launch (start us, length us, event | category | flops | bytes accessed | tf_op | source)
XLA Modules:
  0.0 39.4 jit_solution(1222616159690137824)
XLA Ops:
  0.6 37.8 %ssd_backward.1 = (bf16[1024,256]{1,0:T(8,128)(2,1)S(1)}, bf16[1024,256]{1,0:T(8,128)(2,1)S(1)}, f32[4,1024]{1,0:T(4,128)S(1)}, f32[32,256]{1,0:T(8,128)S(1)}, f...) custom-call(bf16[1024,256]{1,0:T(8,128)(2,1)} %xraw_h.1, bf16[1024,256]{1,0:T(8,128)(2,1)} %zg_h.1, bf16[1024,256]{1,0:T(8,128)(2,1)} %bcr_h.1, ...), custom_call_target="tpu_custom_call" | custom-call | tf_op jit(solution)/shard_map/ssd_backward/pallas_call | solution.py:686
  38.4 1.0 %emit.1 = (bf16[1024,256]{1,0:T(8,128)(2,1)}, bf16[1024,256]{1,0:T(8,128)(2,1)}, f32[4,1024]{1,0:T(4,128)}, f32[32,256]{1,0:T(8,128)}, f32[4,256]{1,0:T(4,128)}, /*index=5*/f32[4,256]{1,0:T(4,128)}) custom-call(bf16[1024,256]{1,0:T(8,128)(2,1)S(1)} %get-tuple-element.12.refs_0_, bf16[1024,256]{1,0:T(8,128)(2,1)S(1)} %get-tuple-element.13.refs_1_, ...), custom_call_target="tpu_custom_call" | custom-call | tf_op jit(solution)/shard_map/emit/pallas_call | solution.py:697

commit v4 on v3

--- a/solution.py
+++ b/solution.py
@@ -73,9 +73,9 @@
 
 def kernel(
     dims, T, W,
-    xraw_h, zg_h, bcr_h, dt_h, a_s, d_s, cvx_h, cvb_h, dout_h,
+    xraw_h, zg_h, bcr_h, dt_h, a_h, d_h, cvx_h, cvb_h, dout_h,
     xg_o, gg_o, sg_o, bg_o, cx_o, cb_o,
-    xraw, zg, bcr, dt, cvx, cvb, dout,
+    xraw, zg, bcr, dt, cvx, cvb, dout, a_s, d_s,
     XF, BCF, XS, BCS, DTE, ENT, LEA, YIN, WGIN, XSL, BS,
     XP, WX, WL, DY, DYE, BCP, MX,
     GC, DC, WP, TOT, LS, NS, SB, GB, EB, SLOT, CR, CSLOT, FS, DEC,
@@ -134,22 +134,23 @@
     loads = [
         pltpu.make_async_copy(a, b, s_in.at[i])
         for i, (a, b) in enumerate(
-            [(dt_h, dt), (zg_h, zg), (dout_h, dout), (bcr_h, bcr), (xraw_h, xraw),
-             (cvx_h, cvx), (cvb_h, cvb)]
+            [(dt_h, dt), (a_h, a_s), (d_h, d_s), (cvb_h, cvb), (cvx_h, cvx),
+             (dout_h, dout), (zg_h, zg), (bcr_h, bcr), (xraw_h, xraw)]
         )
     ]
     for load in loads:
         load.start()
 
     rows16 = lax.broadcasted_iota(jnp.int32, (heads, BLOCK), 0)
-    a_col = by_head([a_s[h] for h in range(heads)], rows16)
     n16 = nb * heads
     ri = lax.broadcasted_iota(jnp.int32, (BLOCK, BLOCK), 0)
     ci = lax.broadcasted_iota(jnp.int32, (BLOCK, BLOCK), 1)
     tri = (ri <= ci).astype(F32).astype(BF16)
     rr = lax.rem(lax.broadcasted_iota(jnp.int32, (3 * n16, W), 0), n16)
     ll = lax.broadcasted_iota(jnp.int32, (3 * n16, W), 1) // HEAD_DIM
-    loads[0].wait()
+    for load in loads[:3]:
+        load.wait()
+    a_col = by_head([a_s[h] for h in range(heads)], rows16)
     for k in range(nb):
         piece = dt[:, k * BLOCK : (k + 1) * BLOCK]
         DC[k * heads : (k + 1) * heads, :] = piece
@@ -179,7 +180,7 @@
     CH = 64
     N = W // 2
     per = BLOCK // CH
-    for load in loads[1:]:
+    for load in loads[3:8]:
         load.wait()
     XF[0:8, :] = jnp.zeros((8, W), F32)
     BCF[0:8, :] = jnp.zeros((8, W), F32)
@@ -191,7 +192,6 @@
         DY[r, :] = dy
         DYE[r, :] = (dy.astype(F32) * ENT[r, :]).astype(BF16)
         shifted = window(8 + i * CH, CH)
-        XF[shifted, :] = xraw[r, :].astype(F32)
         BCF[shifted, :] = bcr[r, :].astype(F32)
         return carry
 
@@ -235,6 +235,7 @@
 
     pl.semaphore_wait(barrier, nseq * nc - 1 + nzy - 1)
 
+    loads[8].wait()
     halo_x = send(xraw.at[T - 16 :], HXR, s_h.at[0], r_h.at[0], at_seq(s + 1))
     halo_b = send(bcr.at[T - 16 :], HBR, s_h.at[1], r_h.at[1], at_seq(s + 1))
 
@@ -257,7 +258,11 @@
         def _():
             state_copy(d).start()
 
-    loop(0, T // CH, conv_x_chunk, 0, 2)
+    def widen(i, carry):
+        XF[window(8 + i * CH, CH), :] = xraw[blk(i, CH), :].astype(F32)
+        return conv_x_chunk(i, carry)
+
+    loop(0, T // CH, widen, 0, 2)
     ends = [mm(BCP[blk(k), :N], WL[blk(k), :], TN) for k in range(nb)]
     state = jnp.zeros((N, W), F32)
     for k in range(nb):
@@ -523,24 +528,7 @@
         def _():
             z_copy(d).start()
 
-    @pl.when(s < nseq - 1)
-    def _():
-        halo_bs.wait_recv()
-        BS[T : T + 8, :] = HSB[1]
-
-    @pl.when(s == nseq - 1)
-    def _():
-        BS[T : T + 8, :] = jnp.zeros((8, W), F32)
-
-    adjoint_piece(2)
     sums = block_channels(1, sums)
-    a_copy(2).wait_recv()
-    pair_sum(nzy - 1, 0)
-
-    @pl.when(m < nzy - 1)
-    def _():
-        z_copy(nzy - 1 - m).start()
-
     sums = block_channels(2, sums)
     sums = block_channels(3, sums)
     CXS[s] = stack_taps(sums)
@@ -552,20 +540,6 @@
         for p in range(1, n):
             out = out + buf[p]
         return out
-
-    for d in range(1, nzy):
-        t = other_zy(d)
-        send(CBZ.at[t], CBZ.at[t], s_cz.at[d], r_cz.at[t], at_zy(t)).wait_recv()
-    mine = s * nc + c
-    CBS[mine] = total(CBZ, nzy)
-
-    def sc_copy(d):
-        p, _ = other(d // 2)
-        dev = at_seq(p) if d % 2 == 0 else {**at_seq(p), **core_dev}
-        return send(CBS.at[mine], CBS.at[mine], s_cb.at[d], r_cb.at[mine], dev)
-
-    for d in range(1, nseq * nc):
-        sc_copy(d).start()
 
     def outputs(i, carry):
         r = blk(i, CH)
@@ -575,7 +549,39 @@
         gg_o[r, :] = (gate * y).astype(BF16)
         return carry
 
-    loop(0, T // CH, outputs, 0, 4)
+    @pl.when(s < nseq - 1)
+    def _():
+        halo_bs.wait_recv()
+        BS[T : T + 8, :] = HSB[1]
+
+    @pl.when(s == nseq - 1)
+    def _():
+        BS[T : T + 8, :] = jnp.zeros((8, W), F32)
+
+    adjoint_piece(2)
+    loop(0, T // CH // 2, outputs, 0, 4)
+    for d in range(1, nzy):
+        t = other_zy(d)
+        send(CBZ.at[t], CBZ.at[t], s_cz.at[d], r_cz.at[t], at_zy(t)).wait_recv()
+    mine = s * nc + c
+    CBS[mine] = total(CBZ, nzy)
+
+    def sc_copy(d):
+        p, _ = other(d // 2)
+        dev = at_seq(p) if d % 2 == 0 else {**at_seq(p), **core_dev}
+        return send(CBS.at[mine], CBS.at[mine], s_cb.at[d], r_cb.at[mine], dev)
+
+    for d in range(1, nseq * nc):
+        sc_copy(d).start()
+
+    a_copy(2).wait_recv()
+    pair_sum(nzy - 1, 0)
+
+    @pl.when(m < nzy - 1)
+    def _():
+        z_copy(nzy - 1 - m).start()
+
+    loop(T // CH // 2, T // CH, outputs, 0, 4)
 
     def x_adjoint(i, carry):
         r = blk(i, CH)
@@ -659,6 +665,7 @@
     dma = lambda n: pltpu.SemaphoreType.DMA((n,))
     scratch = (
         [half, half, half, vm(heads, T, F32), taps, taps, half]
+        + [pltpu.SMEM((heads,), F32)] * 2
         + [ext, ext] + [full] * 7 + [ext, ext]
         + [half] * 5 + [half, vm(T, BLOCK, BF16)]
         + [vm(nb * heads, BLOCK, F32), vm(nb * heads, BLOCK, F32), vm(3 * nb * heads, BLOCK, BF16)]
@@ -674,11 +681,10 @@
         + [vm(nzy, nc, own, W, BF16), vm(nzy, own, W, BF16)]
         + [vm(nzy, own, W, BF16)] * 2
         + [vm(nseq, TAPS, W, F32), vm(nseq * nc, TAPS, W, F32), vm(nzy, TAPS, W, F32)]
-        + [dma(7)] + [dma(2)] * 2 + [dma(nseq)] * 4 + [dma(2)] * 2 + [dma(3)] * 2 + [dma(nzy)] * 2
+        + [dma(9)] + [dma(2)] * 2 + [dma(nseq)] * 4 + [dma(2)] * 2 + [dma(3)] * 2 + [dma(nzy)] * 2
         + [dma(nseq)] * 2 + [dma(nseq * nc)] * 2 + [dma(nzy)] * 2
     )
     vspec = pl.BlockSpec(memory_space=pltpu.VMEM)
-    sspec = pl.BlockSpec(memory_space=pltpu.SMEM)
     hspec = pl.BlockSpec(memory_space=pltpu.HBM)
     shapes = [
         ((T, W), BF16), ((T, W), BF16), ((heads, T), F32), ((own, W), F32), ((TAPS, W), F32), ((TAPS, W), F32),
@@ -687,7 +693,7 @@
         functools.partial(kernel, dims, T, W),
         name="ssd_backward",
         out_shape=tuple(pltpu.VMEM(*sh) for sh in shapes),
-        in_specs=[hspec, hspec, hspec, hspec, sspec, sspec, hspec, hspec, hspec],
+        in_specs=[hspec] * 9,
         out_specs=tuple([vspec] * 6),
         scratch_shapes=scratch,
         compiler_params=pltpu.CompilerParams(

time: 39.6 us -> 39 us (0.985)
  Pallas kernels: 38.8 us -> 38.2 us
    pallas_call x1, Pallas kernels: 37.8 us -> 37.2 us  [local(): pl.pallas_call(functools.partial(kernel, dims, T, W), name='ssd_backward'...]
where the time goes in v4:
time: 39 us; the launch traced here: 38.9 us
  Pallas kernels  38.2 us (98%)
  between operations  0.64 us (2%)
    pallas_call x1, Pallas kernels, local(): pl.pallas_call(functools.partial(kernel, dims, T, W), name='ssd_backward'...  37.2 us
    pallas_call x1, Pallas kernels, local(): pl.pallas_call(emit, name='emit', out_shape=tuple((jax.ShapeDtypeStruct(*...  1.03 us

profile of v4, /device:TPU:1, one launch (start us, length us, event | category | flops | bytes accessed | tf_op | source)
XLA Modules:
  0.0 38.9 jit_solution(12846840143755363612)
XLA Ops:
  0.6 37.2 %ssd_backward.1 = (bf16[1024,256]{1,0:T(8,128)(2,1)S(1)}, bf16[1024,256]{1,0:T(8,128)(2,1)S(1)}, f32[4,1024]{1,0:T(4,128)S(1)}, f32[32,256]{1,0:T(8,128)S(1)}, f...) custom-call(bf16[1024,256]{1,0:T(8,128)(2,1)} %xraw_h.1, bf16[1024,256]{1,0:T(8,128)(2,1)} %zg_h.1, bf16[1024,256]{1,0:T(8,128)(2,1)} %bcr_h.1, ...), custom_call_target="tpu_custom_call" | custom-call | tf_op jit(solution)/shard_map/ssd_backward/pallas_call | solution.py:692
  37.8 1.0 %emit.1 = (bf16[1024,256]{1,0:T(8,128)(2,1)}, bf16[1024,256]{1,0:T(8,128)(2,1)}, f32[4,1024]{1,0:T(4,128)}, f32[32,256]{1,0:T(8,128)}, f32[4,256]{1,0:T(4,128)}, /*index=5*/f32[4,256]{1,0:T(4,128)}) custom-call(bf16[1024,256]{1,0:T(8,128)(2,1)S(1)} %get-tuple-element.12.refs_0_, bf16[1024,256]{1,0:T(8,128)(2,1)S(1)} %get-tuple-element.13.refs_1_, ...), custom_call_target="tpu_custom_call" | custom-call | tf_op jit(solution)/shard_map/emit/pallas_call | solution.py:703

commit v5 on v4

--- a/solution.py
+++ b/solution.py
@@ -110,6 +110,8 @@
 
     far_first = sorted(range(1, nzy), key=lambda d: -min(d, nzy - d))
 
+    seq_far = sorted(range(1, nseq), key=lambda d: -min(d, nseq - d))
+
     def send(src, dst, ss, rs, dev):
         return pltpu.make_async_remote_copy(
             src_ref=src, dst_ref=dst, send_sem=ss, recv_sem=rs,
@@ -252,7 +254,7 @@
         p, wrapped = other(d)
         return send(CR.at[wrapped], CSLOT.at[s], s_cr.at[d], r_cr.at[s], at_seq(p))
 
-    for d in sorted(range(1, nseq), key=lambda d: -min(d, nseq - d)):
+    for d in seq_far:
 
         @pl.when(s + d >= nseq)
         def _():
@@ -269,7 +271,7 @@
         LS[k] = state
         state = jnp.exp(-TOT[k][0:1, :]) * state + ends[k]
     EB[0] = state.astype(BF16)
-    for d in sorted(range(1, nseq), key=lambda d: -min(d, nseq - d)):
+    for d in seq_far:
 
         @pl.when(s + d < nseq)
         def _():
@@ -355,7 +357,7 @@
     first = jnp.where(edge, BCP[0:16, :], jnp.zeros((16, W), BF16))
     CR[0, :, W:] = first[:, :N]
     CR[1, :, W:] = first[:, N:]
-    for d in range(1, nseq):
+    for d in seq_far:
         edge_copy(d).start()
     start0 = mm(first[:, :N], WL[0:16, :], TN)
 
@@ -571,8 +573,10 @@
         dev = at_seq(p) if d % 2 == 0 else {**at_seq(p), **core_dev}
         return send(CBS.at[mine], CBS.at[mine], s_cb.at[d], r_cb.at[mine], dev)
 
-    for d in range(1, nseq * nc):
-        sc_copy(d).start()
+    for d in seq_far:
+        sc_copy(2 * d + 1).start()
+        sc_copy(2 * d).start()
+    sc_copy(1).start()
 
     a_copy(2).wait_recv()
     pair_sum(nzy - 1, 0)

time: 39 us -> 38.4 us (0.985)
  Pallas kernels: 38.2 us -> 37.6 us
    pallas_call x1, Pallas kernels: 37.2 us -> 36.6 us  [local(): pl.pallas_call(functools.partial(kernel, dims, T, W), name='ssd_backward'...]
where the time goes in v5:
time: 38.4 us; the launch traced here: 38.3 us
  Pallas kernels  37.6 us (98%)
  between operations  0.64 us (2%)
    pallas_call x1, Pallas kernels, local(): pl.pallas_call(functools.partial(kernel, dims, T, W), name='ssd_backward'...  36.6 us
    pallas_call x1, Pallas kernels, local(): pl.pallas_call(emit, name='emit', out_shape=tuple((jax.ShapeDtypeStruct(*...  1.03 us

profile of v5, /device:TPU:1, one launch (start us, length us, event | category | flops | bytes accessed | tf_op | source)
XLA Modules:
  0.0 38.3 jit_solution(17381414895970400368)
XLA Ops:
  0.6 36.6 %ssd_backward.1 = (bf16[1024,256]{1,0:T(8,128)(2,1)S(1)}, bf16[1024,256]{1,0:T(8,128)(2,1)S(1)}, f32[4,1024]{1,0:T(4,128)S(1)}, f32[32,256]{1,0:T(8,128)S(1)}, f...) custom-call(bf16[1024,256]{1,0:T(8,128)(2,1)} %xraw_h.1, bf16[1024,256]{1,0:T(8,128)(2,1)} %zg_h.1, bf16[1024,256]{1,0:T(8,128)(2,1)} %bcr_h.1, ...), custom_call_target="tpu_custom_call" | custom-call | tf_op jit(solution)/shard_map/ssd_backward/pallas_call | solution.py:696
  37.2 1.0 %emit.1 = (bf16[1024,256]{1,0:T(8,128)(2,1)}, bf16[1024,256]{1,0:T(8,128)(2,1)}, f32[4,1024]{1,0:T(4,128)}, f32[32,256]{1,0:T(8,128)}, f32[4,256]{1,0:T(4,128)}, /*index=5*/f32[4,256]{1,0:T(4,128)}) custom-call(bf16[1024,256]{1,0:T(8,128)(2,1)S(1)} %get-tuple-element.12.refs_0_, bf16[1024,256]{1,0:T(8,128)(2,1)S(1)} %get-tuple-element.13.refs_1_, ...), custom_call_target="tpu_custom_call" | custom-call | tf_op jit(solution)/shard_map/emit/pallas_call | solution.py:707
